TPU v7x, 32 devices: a whole 2x2x4 slice. The times are simulated.
32 devices in a mesh: rep: 2 (over x), fsdp: 4 (over z), ns: 4 (over y, core).
Axes of the slice: x: 2, y: 2, z: 4, core: 2. Of those that a mesh axis runs over, the one named last changes fastest.
Arguments:
- tokens: bfloat16 [8192, 2048], P(('rep', 'fsdp', 'ns')), may hold values from -6 to 6
- cotangent: bfloat16 [8192, 2048], P(('rep', 'fsdp', 'ns')), may hold values from -6 to 6
- placement: int32 [8192], P(('rep', 'fsdp', 'ns')), may hold values from 0 to 8191, as said below
- lengths: int32 [2, 4], P('rep'), may hold values from 1 to 2048, 4096 in all within a row
- step_count: int32 [1], replicated, may hold values from 1 to 16
- norm_gain: float32 [2048], replicated, may hold values from 0.5 to 1.5
- norm_bias: float32 [2048], replicated, may hold values from -1.25 to 1.25
- project_weight: float32 [2048, 6144], P('fsdp', 'ns'), may hold values from -0.125 to 0.125
- project_bias: float32 [6144], P('ns'), may hold values from -1.25 to 1.25
- output_weight: float32 [2048, 2048], P('ns', 'fsdp'), may hold values from -1.5 to 1.5
- output_bias: float32 [2048], replicated, may hold values from -1.25 to 1.25
- expand_weight: float32 [2048, 8192], P('fsdp', 'ns'), may hold values from -0.125 to 0.125
- expand_bias: float32 [8192], P('ns'), may hold values from -1.25 to 1.25
- reduce_weight: float32 [8192, 2048], P('ns', 'fsdp'), may hold values from -0.0625 to 0.0625
- reduce_bias: float32 [2048], replicated, may hold values from -1.25 to 1.25
- project_momentum: float32 [2048, 6144], P('fsdp', 'ns'), may hold values from -512 to 512
- output_momentum: float32 [2048, 2048], P('ns', 'fsdp'), may hold values from -28 to 28
- expand_momentum: float32 [2048, 8192], P('fsdp', 'ns'), may hold values from -160 to 160
- reduce_momentum: float32 [8192, 2048], P('ns', 'fsdp'), may hold values from -256 to 256
- norm_gain_first: float32 [2048], replicated, may hold values from -64 to 64
- norm_gain_second: float32 [2048], replicated, may hold values from 409.6 to 1638.4
- norm_bias_first: float32 [2048], replicated, may hold values from -64 to 64
- norm_bias_second: float32 [2048], replicated, may hold values from 409.6 to 1638.4
- project_bias_first: float32 [6144], P('ns'), may hold values from -64 to 64
- project_bias_second: float32 [6144], P('ns'), may hold values from 409.6 to 1638.4
- output_bias_first: float32 [2048], replicated, may hold values from -64 to 64
- output_bias_second: float32 [2048], replicated, may hold values from 409.6 to 1638.4
- expand_bias_first: float32 [8192], P('ns'), may hold values from -64 to 64
- expand_bias_second: float32 [8192], P('ns'), may hold values from 409.6 to 1638.4
- reduce_bias_first: float32 [2048], replicated, may hold values from -64 to 64
- reduce_bias_second: float32 [2048], replicated, may hold values from 409.6 to 1638.4
Outputs:
- layer_output: bfloat16 [8192, 2048], P(('rep', 'fsdp', 'ns'))
- input_grad: bfloat16 [8192, 2048], P(('rep', 'fsdp', 'ns'))
- norm_gain_grad: float32 [2048], replicated
- norm_bias_grad: float32 [2048], replicated
- project_weight_grad: float32 [2048, 6144], P('fsdp', 'ns')
- project_bias_grad: float32 [6144], P('ns')
- output_weight_grad: float32 [2048, 2048], P('ns', 'fsdp')
- output_bias_grad: float32 [2048], replicated
- expand_weight_grad: float32 [2048, 8192], P('fsdp', 'ns')
- expand_bias_grad: float32 [8192], P('ns')
- reduce_weight_grad: float32 [8192, 2048], P('ns', 'fsdp')
- reduce_bias_grad: float32 [2048], replicated
- norm_gain_new: float32 [2048], replicated
- norm_bias_new: float32 [2048], replicated
- project_weight_new: float32 [2048, 6144], P('fsdp', 'ns')
- project_bias_new: float32 [6144], P('ns')
- output_weight_new: float32 [2048, 2048], P('ns', 'fsdp')
- output_bias_new: float32 [2048], replicated
- expand_weight_new: float32 [2048, 8192], P('fsdp', 'ns')
- expand_bias_new: float32 [8192], P('ns')
- reduce_weight_new: float32 [8192, 2048], P('ns', 'fsdp')
- reduce_bias_new: float32 [2048], replicated
- project_weight_copy: bfloat16 [2048, 6144], P('fsdp', 'ns')
- output_weight_copy: bfloat16 [2048, 2048], P('ns', 'fsdp')
- expand_weight_copy: bfloat16 [2048, 8192], P('fsdp', 'ns')
- reduce_weight_copy: bfloat16 [8192, 2048], P('ns', 'fsdp')
- project_momentum_new: float32 [2048, 6144], P('fsdp', 'ns')
- output_momentum_new: float32 [2048, 2048], P('ns', 'fsdp')
- expand_momentum_new: float32 [2048, 8192], P('fsdp', 'ns')
- reduce_momentum_new: float32 [8192, 2048], P('ns', 'fsdp')
- norm_gain_first_new: float32 [2048], replicated
- norm_gain_second_new: float32 [2048], replicated
- norm_bias_first_new: float32 [2048], replicated
- norm_bias_second_new: float32 [2048], replicated
- project_bias_first_new: float32 [6144], P('ns')
- project_bias_second_new: float32 [6144], P('ns')
- output_bias_first_new: float32 [2048], replicated
- output_bias_second_new: float32 [2048], replicated
- expand_bias_first_new: float32 [8192], P('ns')
- expand_bias_second_new: float32 [8192], P('ns')
- reduce_bias_first_new: float32 [2048], replicated
- reduce_bias_second_new: float32 [2048], replicated
Inputs may be any that keep to these rules, and one draw needn't show every extreme that they name: placement is a permutation; it maps the 256 given rows of each device to packed rows of the devices with the same rep and ns index, exactly 64 to each fsdp index, into that device's block of 64 rows that starts at 64 times the sender's fsdp index. Each row of lengths sums to 4096; in each row the largest length is exactly 2048.
All inputs are finite; a program needn't handle non-finite values.
Results may differ from a plain program's by a relative error of at most 0.006.
The roundings to bfloat16 on the way count: a program that leaves them out, or rounds other values in their place, can miss the bound.
Values may be sent and summed in bfloat16 or wider, within the bound.
A program may use at most 384 MiB of HBM per device.

v0:
```python
import math

import jax
import jax.numpy as jnp
from jax import lax
from jax.sharding import PartitionSpec as P

D = 2048
HEAD_DIM = 64
ROT = 32
FF = 8192
SCHULZ_STEPS = 5


NORM_EPSILON = 1e-05
ROPE_BASE = 10000.0
NEG_LARGE = -1e30
SCHULZ_FIRST = 3.4445
SCHULZ_SECOND = -4.775
SCHULZ_THIRD = 2.0315
SCHULZ_EPSILON = 1e-06
MUON_RATE = 0.2
MUON_DECAY = 0.5
RMS_MATCH = 0.2
WEIGHT_DECAY = 0.1
ADAM_RATE = 0.2
ADAM_FIRST = 0.9
ADAM_SECOND = 0.95
ADAM_EPSILON = 1e-08


def sequence_layout(row_lengths, row_ids):
    offsets = jnp.cumsum(row_lengths) - row_lengths
    covered = row_ids[:, None] >= offsets[None, :]
    seq_ids = jnp.sum(covered.astype(jnp.int32), axis=1) - 1
    starts = jnp.max(jnp.where(covered, offsets[None, :], 0), axis=1)
    return (seq_ids, starts)


def rope_tables(positions):
    half_width = ROT // 2
    inverse = jnp.power(ROPE_BASE, -jnp.arange(half_width, dtype=jnp.float32) * (2.0 / ROT))
    angles = positions.astype(jnp.float32)[:, None] * inverse[None, :]
    return (jnp.cos(angles), jnp.sin(angles))


def rotate(vectors, cosine, sine):
    half_width = ROT // 2
    leading = vectors[..., :half_width]
    trailing = vectors[..., half_width:ROT]
    cosine_rows = cosine[:, None, :]
    sine_rows = sine[:, None, :]
    return jnp.concatenate(
        [
            leading * cosine_rows - trailing * sine_rows,
            trailing * cosine_rows + leading * sine_rows,
            vectors[..., ROT:],
        ],
        axis=-1,
    )


def layer_norm(rows_in, gain_vector, shift_vector):
    row_mean = jnp.mean(rows_in, axis=1, keepdims=True)
    centred = rows_in - row_mean
    row_var = jnp.mean(centred * centred, axis=1, keepdims=True)
    return centred * lax.rsqrt(row_var + NORM_EPSILON) * gain_vector + shift_vector


def gelu_tanh(values_in):
    return jax.nn.gelu(values_in, approximate=True)


def local_gram(block_part):
    return jnp.einsum("ik,jk->ij", block_part, block_part, precision=lax.Precision.HIGHEST)


def schulz_turn(block_part, gram_sum):
    mixing = SCHULZ_SECOND * gram_sum + SCHULZ_THIRD * jnp.dot(
        gram_sum, gram_sum, precision=lax.Precision.HIGHEST
    )
    return SCHULZ_FIRST * block_part + jnp.dot(mixing, block_part, precision=lax.Precision.HIGHEST)


def muon_weight(weight, ortho, long_side):
    return weight - MUON_RATE * (RMS_MATCH * math.sqrt(long_side) * ortho + WEIGHT_DECAY * weight)


def adam_update(param, first_moment, second_moment, gradient, step_count):
    moment_one = ADAM_FIRST * first_moment + (1.0 - ADAM_FIRST) * gradient
    moment_two = ADAM_SECOND * second_moment + (1.0 - ADAM_SECOND) * gradient * gradient
    step_value = step_count[0].astype(jnp.float32)
    one_fixed = moment_one / (1.0 - ADAM_FIRST**step_value)
    two_fixed = moment_two / (1.0 - ADAM_SECOND**step_value)
    param_new = param - ADAM_RATE * one_fixed / (jnp.sqrt(two_fixed) + ADAM_EPSILON)
    return (param_new, moment_one, moment_two)


def per_device(
    tokens,
    cotangent,
    placement,
    lengths,
    step_count,
    norm_gain,
    norm_bias,
    project_weight,
    project_bias,
    output_weight,
    output_bias,
    expand_weight,
    expand_bias,
    reduce_weight,
    reduce_bias,
    project_momentum,
    output_momentum,
    expand_momentum,
    reduce_momentum,
    norm_gain_first,
    norm_gain_second,
    norm_bias_first,
    norm_bias_second,
    project_bias_first,
    project_bias_second,
    output_bias_first,
    output_bias_second,
    expand_bias_first,
    expand_bias_second,
    reduce_bias_first,
    reduce_bias_second,
):
    fsdp_count = lax.axis_size("fsdp")
    ns_count = lax.axis_size("ns")
    shard_rows = tokens.shape[0]
    slot_rows = shard_rows // fsdp_count
    group_rows = shard_rows * ns_count
    pack_rows = group_rows * fsdp_count
    fsdp_at = lax.axis_index("fsdp")
    ns_at = lax.axis_index("ns")
    row_lengths = lengths[0]
    heads_here = project_bias.shape[0] // (3 * HEAD_DIM)
    head_cols = heads_here * HEAD_DIM
    scale_factor = HEAD_DIM ** (-0.5)
    within = placement % shard_rows
    dest_fsdp = placement // shard_rows // ns_count % fsdp_count
    slot_index = dest_fsdp * slot_rows + within - fsdp_at * slot_rows
    source_row = (
        jnp.zeros((shard_rows,), jnp.int32)
        .at[slot_index]
        .set(jnp.arange(shard_rows, dtype=jnp.int32))
    )
    dealt_tokens, dealt_cotangent = (
        lax.all_to_all(tokens[source_row], "fsdp", split_axis=0, concat_axis=0, tiled=True),
        lax.all_to_all(cotangent[source_row], "fsdp", split_axis=0, concat_axis=0, tiled=True),
    )
    token_rows = dealt_tokens.astype(jnp.float32)
    normed, norm_back = jax.vjp(layer_norm, token_rows, norm_gain, norm_bias)
    normed_low = normed.astype(jnp.bfloat16)
    normed_all, cotangent_all = (
        lax.all_gather(normed_low, "ns", axis=0, tiled=True),
        lax.all_gather(dealt_cotangent, "ns", axis=0, tiled=True),
    )
    project_low = project_weight.astype(jnp.bfloat16)
    output_low = output_weight.astype(jnp.bfloat16)
    expand_low = expand_weight.astype(jnp.bfloat16)
    reduce_low = reduce_weight.astype(jnp.bfloat16)
    project_full, output_full, expand_full, reduce_full = (
        lax.all_gather(project_low, "fsdp", axis=0, tiled=True),
        lax.all_gather(output_low, "fsdp", axis=1, tiled=True),
        lax.all_gather(expand_low, "fsdp", axis=0, tiled=True),
        lax.all_gather(reduce_low, "fsdp", axis=1, tiled=True),
    )
    group_first = fsdp_at * group_rows
    query_rows = group_first + jnp.arange(group_rows, dtype=jnp.int32)
    query_seq, query_starts = sequence_layout(row_lengths, query_rows)
    positions = query_rows - query_starts
    reach_first = query_starts[0]
    query_last = group_first + group_rows - 1
    cosine, sine = rope_tables(positions)
    joined = jnp.dot(normed_all, project_full, preferred_element_type=jnp.float32) + project_bias
    joined = joined.reshape(group_rows, heads_here, 3, HEAD_DIM)
    query_view = rotate(joined[:, :, 0], cosine, sine).astype(jnp.bfloat16)
    keys_here = (
        rotate(joined[:, :, 1], cosine, sine).astype(jnp.bfloat16).reshape(group_rows, head_cols)
    )
    values_here = joined[:, :, 2].astype(jnp.bfloat16).reshape(group_rows, head_cols)
    paired_here = jnp.stack([keys_here, values_here], axis=1)

    def wanted(key_first, key_count):
        return (key_first <= query_last) & (key_first + key_count - 1 >= reach_first)

    def piece_scores(key_piece, key_first):
        key_count = key_piece.shape[0]
        key_rows = key_first + jnp.arange(key_count, dtype=jnp.int32)
        key_seq = sequence_layout(row_lengths, key_rows)[0]
        scores = (
            jnp.einsum(
                "qhe,khe->hqk",
                query_view,
                key_piece.reshape(key_count, heads_here, HEAD_DIM),
                preferred_element_type=jnp.float32,
            )
            * scale_factor
        )
        allowed = (key_seq[None, :] == query_seq[:, None]) & (
            key_rows[None, :] <= query_rows[:, None]
        )
        return jnp.where(allowed[None], scores, NEG_LARGE)

    paired_group = lax.all_gather(paired_here, "fsdp", axis=0, tiled=True)
    paired_stack = paired_group.reshape(fsdp_count, group_rows, 2, head_cols)
    first_rows = jnp.arange(fsdp_count, dtype=jnp.int32) * group_rows

    def sweep(step_fn, initial):

        def scan_body(running, scan_item):
            return step_fn(running, scan_item[0][:, 0], scan_item[0][:, 1], scan_item[1])

        return lax.scan(scan_body, initial, (paired_stack, first_rows))

    def stats_step(running, key_piece, value_piece, key_first):

        def stats_compute(held_stats):
            row_top, row_sum = held_stats
            scores = piece_scores(key_piece, key_first)
            top_new = jnp.maximum(row_top, jnp.max(scores, axis=2))
            sum_new = row_sum * jnp.exp(row_top - top_new) + jnp.sum(
                jnp.exp(scores - top_new[:, :, None]), axis=2
            )
            return (top_new, sum_new)

        return (
            lax.cond(
                wanted(key_first, key_piece.shape[0]),
                stats_compute,
                lambda held_stats: held_stats,
                running,
            ),
            None,
        )

    initial_stats = (
        jnp.full((heads_here, group_rows), NEG_LARGE, jnp.float32),
        jnp.zeros((heads_here, group_rows), jnp.float32),
    )
    final_stats = sweep(stats_step, initial_stats)[0]
    log_total = final_stats[0] + jnp.log(final_stats[1])

    def output_step(running, key_piece, value_piece, key_first):
        key_count = key_piece.shape[0]

        def output_compute(accum):
            scores = piece_scores(key_piece, key_first)
            probs_low = jnp.exp(scores - log_total[:, :, None]).astype(jnp.bfloat16)
            return accum + jnp.einsum(
                "hqk,khe->qhe",
                probs_low,
                value_piece.reshape(key_count, heads_here, HEAD_DIM),
                preferred_element_type=jnp.float32,
            )

        return (
            lax.cond(wanted(key_first, key_count), output_compute, lambda accum: accum, running),
            None,
        )

    attended = sweep(output_step, jnp.zeros((group_rows, heads_here, HEAD_DIM), jnp.float32))[0]
    attended_low = attended.reshape(group_rows, head_cols).astype(jnp.bfloat16)
    hidden = jnp.dot(normed_all, expand_full, preferred_element_type=jnp.float32) + expand_bias
    activated, gelu_back = jax.vjp(gelu_tanh, hidden)
    activated_low = activated.astype(jnp.bfloat16)
    branch_sum = lax.psum_scatter(
        jnp.dot(attended_low, output_full, preferred_element_type=jnp.float32)
        + jnp.dot(activated_low, reduce_full, preferred_element_type=jnp.float32),
        "ns",
        scatter_dimension=0,
        tiled=True,
    )
    layer_rows = (token_rows + branch_sum + output_bias + reduce_bias).astype(jnp.bfloat16)
    back_project, back_output, back_expand, back_reduce = (
        lax.all_gather(project_low, "fsdp", axis=0, tiled=True),
        lax.all_gather(output_low, "fsdp", axis=1, tiled=True),
        lax.all_gather(expand_low, "fsdp", axis=0, tiled=True),
        lax.all_gather(reduce_low, "fsdp", axis=1, tiled=True),
    )
    d_attended = jnp.einsum(
        "td,hd->th", cotangent_all, back_output, preferred_element_type=jnp.float32
    ).astype(jnp.bfloat16)
    d_attended_view = d_attended.reshape(group_rows, heads_here, HEAD_DIM)
    d_activated = jnp.einsum(
        "td,fd->tf", cotangent_all, back_reduce, preferred_element_type=jnp.float32
    )
    d_hidden = gelu_back(d_activated)[0].astype(jnp.bfloat16)

    def delta_step(running, key_piece, value_piece, key_first):
        key_count = key_piece.shape[0]

        def delta_compute(accum):
            scores = piece_scores(key_piece, key_first)
            probs = jnp.exp(scores - log_total[:, :, None])
            d_probs = jnp.einsum(
                "qhe,khe->hqk",
                d_attended_view,
                value_piece.reshape(key_count, heads_here, HEAD_DIM),
                preferred_element_type=jnp.float32,
            )
            return accum + jnp.sum(probs * d_probs, axis=2)

        return (
            lax.cond(wanted(key_first, key_count), delta_compute, lambda accum: accum, running),
            None,
        )

    delta = sweep(delta_step, jnp.zeros((heads_here, group_rows), jnp.float32))[0]

    def grads_step(running, key_piece, value_piece, key_first):
        key_count = key_piece.shape[0]

        def grads_compute(d_queries):
            keys_view = key_piece.reshape(key_count, heads_here, HEAD_DIM)
            values_view = value_piece.reshape(key_count, heads_here, HEAD_DIM)
            scores = piece_scores(key_piece, key_first)
            probs = jnp.exp(scores - log_total[:, :, None])
            d_probs = jnp.einsum(
                "qhe,khe->hqk", d_attended_view, values_view, preferred_element_type=jnp.float32
            )
            d_scores = (probs * (d_probs - delta[:, :, None])).astype(jnp.bfloat16)
            d_queries = (
                d_queries
                + jnp.einsum(
                    "hqk,khe->qhe", d_scores, keys_view, preferred_element_type=jnp.float32
                )
                * scale_factor
            )
            d_keys = (
                jnp.einsum("hqk,qhe->khe", d_scores, query_view, preferred_element_type=jnp.float32)
                * scale_factor
            )
            d_values = jnp.einsum(
                "hqk,qhe->khe",
                probs.astype(jnp.bfloat16),
                d_attended_view,
                preferred_element_type=jnp.float32,
            )
            return (
                d_queries,
                jnp.stack(
                    [d_keys.reshape(key_count, head_cols), d_values.reshape(key_count, head_cols)],
                    axis=1,
                ),
            )

        def skipped(d_queries):
            return (d_queries, jnp.zeros((key_count, 2, head_cols), jnp.float32))

        return lax.cond(wanted(key_first, key_count), grads_compute, skipped, running)

    d_queries, key_extras = sweep(
        grads_step, jnp.zeros((group_rows, heads_here, HEAD_DIM), jnp.float32)
    )
    key_sums = lax.psum_scatter(
        key_extras.reshape(pack_rows, 2, head_cols), "fsdp", scatter_dimension=0, tiled=True
    )
    d_keys_own = key_sums[:, 0].reshape(group_rows, heads_here, HEAD_DIM)
    d_values_own = key_sums[:, 1].reshape(group_rows, heads_here, HEAD_DIM)
    d_joined = jnp.stack(
        [rotate(d_queries, cosine, -sine), rotate(d_keys_own, cosine, -sine), d_values_own], axis=2
    )
    d_joined = d_joined.reshape(group_rows, 3 * head_cols).astype(jnp.bfloat16)
    d_normed = lax.psum_scatter(
        jnp.einsum("tc,dc->td", d_joined, back_project, preferred_element_type=jnp.float32)
        + jnp.einsum("tf,df->td", d_hidden, back_expand, preferred_element_type=jnp.float32),
        "ns",
        scatter_dimension=0,
        tiled=True,
    )
    d_tokens_norm, gain_term, shift_term = norm_back(d_normed)
    input_rows = (dealt_cotangent.astype(jnp.float32) + d_tokens_norm).astype(jnp.bfloat16)
    back_layer, back_input = (
        lax.all_to_all(layer_rows, "fsdp", split_axis=0, concat_axis=0, tiled=True),
        lax.all_to_all(input_rows, "fsdp", split_axis=0, concat_axis=0, tiled=True),
    )
    layer_output = back_layer[slot_index]
    input_grad = back_input[slot_index]
    project_term = jnp.einsum("td,tc->dc", normed_all, d_joined, preferred_element_type=jnp.float32)
    output_term = jnp.einsum(
        "th,td->hd", attended_low, cotangent_all, preferred_element_type=jnp.float32
    )
    expand_term = jnp.einsum("td,tf->df", normed_all, d_hidden, preferred_element_type=jnp.float32)
    reduce_term = jnp.einsum(
        "tf,td->fd", activated_low, cotangent_all, preferred_element_type=jnp.float32
    )
    shards = (
        lax.psum_scatter(project_term, "fsdp", scatter_dimension=0, tiled=True),
        lax.psum_scatter(output_term, "fsdp", scatter_dimension=1, tiled=True),
        lax.psum_scatter(expand_term, "fsdp", scatter_dimension=0, tiled=True),
        lax.psum_scatter(reduce_term, "fsdp", scatter_dimension=1, tiled=True),
    )
    project_grad, output_grad, expand_grad, reduce_grad = lax.psum(
        (shards[0], shards[1], shards[2], shards[3]), "rep"
    )
    project_bias_width = project_bias.shape[0]
    expand_bias_width = expand_bias.shape[0]
    project_bias_part = lax.dynamic_update_slice(
        jnp.zeros((project_bias_width * ns_count,), jnp.float32),
        jnp.sum(d_joined, axis=0, dtype=jnp.float32),
        (ns_at * project_bias_width,),
    )
    expand_bias_part = lax.dynamic_update_slice(
        jnp.zeros((expand_bias_width * ns_count,), jnp.float32),
        jnp.sum(d_hidden, axis=0, dtype=jnp.float32),
        (ns_at * expand_bias_width,),
    )
    cotangent_sum = jnp.sum(dealt_cotangent, axis=0, dtype=jnp.float32)
    gain_grad, shift_grad, cotangent_total, project_bias_all, expand_bias_all = lax.psum(
        (gain_term, shift_term, cotangent_sum, project_bias_part, expand_bias_part),
        ("rep", "fsdp", "ns"),
    )
    project_bias_grad = lax.dynamic_slice_in_dim(
        project_bias_all, ns_at * project_bias_width, project_bias_width
    )
    expand_bias_grad = lax.dynamic_slice_in_dim(
        expand_bias_all, ns_at * expand_bias_width, expand_bias_width
    )
    project_mom = MUON_DECAY * project_momentum + project_grad
    output_mom = MUON_DECAY * output_momentum + output_grad
    expand_mom = MUON_DECAY * expand_momentum + expand_grad
    reduce_mom = MUON_DECAY * reduce_momentum + reduce_grad
    current = (project_mom, output_mom.T, expand_mom, reduce_mom.T)
    for turn_id in range(SCHULZ_STEPS):
        grams = lax.psum(
            (
                local_gram(current[0]),
                local_gram(current[1]),
                local_gram(current[2]),
                local_gram(current[3]),
            ),
            "ns",
        )
        if turn_id == 0:
            factors = [lax.rsqrt(jnp.trace(gram_sum) + SCHULZ_EPSILON) for gram_sum in grams]
            current = tuple(
                (block_part * factor_now for block_part, factor_now in zip(current, factors))
            )
            grams = tuple(
                (
                    gram_sum * (factor_now * factor_now)
                    for gram_sum, factor_now in zip(grams, factors)
                )
            )
        current = tuple(
            (schulz_turn(block_part, gram_sum) for block_part, gram_sum in zip(current, grams))
        )
    project_new = muon_weight(project_weight, current[0], 3 * D)
    output_new = muon_weight(output_weight, current[1].T, D)
    expand_new = muon_weight(expand_weight, current[2], FF)
    reduce_new = muon_weight(reduce_weight, current[3].T, FF)
    gain_new, gain_one, gain_two = adam_update(
        norm_gain, norm_gain_first, norm_gain_second, gain_grad, step_count
    )
    shift_new, shift_one, shift_two = adam_update(
        norm_bias, norm_bias_first, norm_bias_second, shift_grad, step_count
    )
    pbias_new, pbias_one, pbias_two = adam_update(
        project_bias, project_bias_first, project_bias_second, project_bias_grad, step_count
    )
    obias_new, obias_one, obias_two = adam_update(
        output_bias, output_bias_first, output_bias_second, cotangent_total, step_count
    )
    ebias_new, ebias_one, ebias_two = adam_update(
        expand_bias, expand_bias_first, expand_bias_second, expand_bias_grad, step_count
    )
    rbias_new, rbias_one, rbias_two = adam_update(
        reduce_bias, reduce_bias_first, reduce_bias_second, cotangent_total, step_count
    )
    return (
        layer_output,
        input_grad,
        gain_grad,
        shift_grad,
        project_grad,
        project_bias_grad,
        output_grad,
        cotangent_total,
        expand_grad,
        expand_bias_grad,
        reduce_grad,
        cotangent_total,
        gain_new,
        shift_new,
        project_new,
        pbias_new,
        output_new,
        obias_new,
        expand_new,
        ebias_new,
        reduce_new,
        rbias_new,
        project_new.astype(jnp.bfloat16),
        output_new.astype(jnp.bfloat16),
        expand_new.astype(jnp.bfloat16),
        reduce_new.astype(jnp.bfloat16),
        project_mom,
        output_mom,
        expand_mom,
        reduce_mom,
        gain_one,
        gain_two,
        shift_one,
        shift_two,
        pbias_one,
        pbias_two,
        obias_one,
        obias_two,
        ebias_one,
        ebias_two,
        rbias_one,
        rbias_two,
    )


def solution(mesh):
    return jax.shard_map(
        per_device,
        mesh=mesh,
        in_specs=(
            P(("rep", "fsdp", "ns"), None),
            P(("rep", "fsdp", "ns"), None),
            P(("rep", "fsdp", "ns")),
            P("rep", None),
            P(),
            P(),
            P(),
            P("fsdp", "ns"),
            P("ns"),
            P("ns", "fsdp"),
            P(),
            P("fsdp", "ns"),
            P("ns"),
            P("ns", "fsdp"),
            P(),
            P("fsdp", "ns"),
            P("ns", "fsdp"),
            P("fsdp", "ns"),
            P("ns", "fsdp"),
            P(),
            P(),
            P(),
            P(),
            P("ns"),
            P("ns"),
            P(),
            P(),
            P("ns"),
            P("ns"),
            P(),
            P(),
        ),
        out_specs=(
            P(("rep", "fsdp", "ns"), None),
            P(("rep", "fsdp", "ns"), None),
            P(),
            P(),
            P("fsdp", "ns"),
            P("ns"),
            P("ns", "fsdp"),
            P(),
            P("fsdp", "ns"),
            P("ns"),
            P("ns", "fsdp"),
            P(),
            P(),
            P(),
            P("fsdp", "ns"),
            P("ns"),
            P("ns", "fsdp"),
            P(),
            P("fsdp", "ns"),
            P("ns"),
            P("ns", "fsdp"),
            P(),
            P("fsdp", "ns"),
            P("ns", "fsdp"),
            P("fsdp", "ns"),
            P("ns", "fsdp"),
            P("fsdp", "ns"),
            P("ns", "fsdp"),
            P("fsdp", "ns"),
            P("ns", "fsdp"),
            P(),
            P(),
            P(),
            P(),
            P("ns"),
            P("ns"),
            P(),
            P(),
            P("ns"),
            P("ns"),
            P(),
            P(),
        ),
        check_vma=False,
    )
```

profile of v0, /device:TPU:0, one launch (start us, length us, event | category | flops | bytes accessed | tf_op | source)
XLA Modules:
  0.0 3243.5 jit_solution(3828976198522550248)
XLA Ops:
  10.9 31.9 all_to_all.45
  52.1 28.1 all_to_all.46
  81.5 116.0 %all-gather.10.cloned.1.call-done = bf16[2048,1536]{1,0:T(8,128)(2,1)} async-done(((bf16[512,1536]{1,0:T(8,128)(2,1)}), bf16[2048,1536]{1,0:T(8,128)(2,1)}) %all-gather.10.cloned.1.call-update) | async-done | bytes 6291472 | tf_op jit(solution)/shard_map/all_gather | solution.py:168
  197.5 11.8 convolution_add_fusion
  231.3 12.2 all-gather.14.cloned.1.call-done
  243.5 34.7 %all-gather.20.cloned.1.call-done = bf16[1024,2048]{1,0:T(8,128)(2,1)} async-done(((bf16[256,2048]{1,0:T(8,128)(2,1)}), bf16[1024,2048]{1,0:T(8,128)(2,1)}) %all-gather.20.cloned.1.call-update) | async-done | bytes 4194320 | tf_op jit(solution)/shard_map/all_gather | solution.py:161
  285.5 144.3 %all-gather.12.cloned.1.call-done = bf16[4096,2,512]{0,2,1:T(8,128)(2,1)} async-done(((bf16[1024,2,512]{0,2,1:T(8,128)(2,1)}), bf16[4096,2,512]{0,2,1:T(8,128)(2,1)}) %all-gather.12.cloned.1.call-update) | async-done | bytes 8388624 | tf_op jit(solution)/shard_map/all_gather | solution.py:210
  429.9 12.4 copy.177
  442.2 11.6 copy.179
  453.8 42.4 %while.73 = (s32[]{:T(128)}, f32[8,1024]{1,0:T(8,128)S(1)}, f32[8,1024]{1,0:T(8,128)S(1)}, s32[4]{0:T(128)S(1)}, s32[]{:T(128)}, /*index=5*/s32[]{:T(128)}, s32[...) while((s32[]{:T(128)}, f32[8,1024]{1,0:T(8,128)S(1)}, ...), condition=%wide.region_13.14_spmd.clone, body=%wide.region_6.13_spmd.clone.sunk | while | flops 1135638528 | bytes 79118744 | solution.py:219
  456.4 32.1 conditional.12
  460.4 13.8 fusion.8
  474.2 14.3 exponential_reduce_fusion
  496.3 45.0 %while.75 = (s32[]{:T(128)}, f32[8,1024]{1,0:T(8,128)S(1)}, s32[4]{0:T(128)S(1)}, s32[]{:T(128)}, s32[]{:T(128)}, /*index=5*/s32[4]{0:T(128)S(1)}, s32[1024]{0:T...) while((s32[]{:T(128)}, f32[8,1024]{1,0:T(8,128)S(1)}, ...), condition=%wide.region_27.28_spmd.clone, body=%wide.region_21.27_spmd.clone.sunk | while | flops 2192586752 | bytes 82002312 | solution.py:219
  498.9 34.7 %conditional.14 = (f32[8,1024]{1,0:T(8,128)S(1)}) conditional(s32[]{:T(128)} %convert_element_type.300, f32[8,1024]{1,0:T(8,128)S(1)} %get-tuple-element.2301, (s32[]{:T(128)}, s32[4]{0:T(128)S(1)}, s32[1024]{0:T(1024)S(1)}, s32[]{:T(128)}, bf16[4,1024,2,512]{1,3,2,0:T(8,128)(2,1)}, /*index=5*/s32[]{:T(128)}, bf16[1024,8,64]{0,2,1:T(8,128)(2,1)S(1)}, ...), branch_computations={%region_22.22_spmd, %region_23.26_spmd} | conditional | flops 2192586752 | bytes 81997944 | solution.py:310
  503.0 14.6 fusion.154
  517.5 16.0 fusion.21
  542.9 138.0 %while.76 = (s32[]{:T(128)}, f32[1024,8,64]{0,2,1:T(8,128)}, f32[4,1024,2,512]{3,1,0,2:T(8,128)}, s32[4]{0:T(128)S(1)}, s32[]{:T(128)}, /*index=5*/s32[]{:T(128)...) while((s32[]{:T(128)}, f32[1024,8,64]{0,2,1:T(8,128)}, ...), condition=%wide.region_33.34_spmd.clone, body=%wide.region_28.33_spmd.clone.sunk | while | flops 5458376704 | bytes 216155136 | solution.py:219
  545.9 79.8 %conditional.15 = (f32[1024,8,64]{0,2,1:T(8,128)}, f32[1,1024,2,512]{1,3,2,0:T(8,128)}) conditional(s32[]{:T(128)} %convert_element_type.301, f32[1024,8,64]{0,2,1:T(8,128)} %get-tuple-element.2345, (s32[]{:T(128)}, s32[4]{0:T(128)S(1)}, s32[1024]{0:T(1024)S(1)}, s32[]{:T(128)}, bf16[4,1024,2,512]{1,3,2,0:T(8,128)(2,1)}, /*index=5*/s32[]{:T(128)}, ...), branch_computations={%region_29.29_spmd, %region_30.32_spmd} | conditional | flops 5458376704 | bytes 199373008 | solution.py:356
  550.4 13.2 fusion.155
  563.5 20.8 fusion.24
  584.4 9.9 convolution_multiply_fusion
  594.3 16.3 fusion.28
  614.8 10.8 bitcast_add_fusion.1
  682.6 29.7 while.74
  685.1 19.2 conditional.13
  690.2 14.1 bitcast_add_fusion
  721.1 14.5 fusion.156
  735.6 19.4 convert_reduce_fusion.4
  757.0 11.8 fusion.160
  768.9 17.3 fusion.139
  788.4 313.8 %reduce-scatter.10.cloned.1.call-done = f32[1024,2,512]{2,0,1:T(8,128)} async-done(((f32[4096,2,512]{2,0,1:T(8,128)}), f32[1024,2,512]{2,0,1:T(8,128)}) %reduce-scatter.10.cloned.1.call-update) | async-done | bytes 4194320 | tf_op jit(solution)/shard_map/reduce_scatter | solution.py:361
  1118.8 9.6 fusion.158
  1128.4 54.0 %reduce-scatter.16.cloned.1.call-done = f32[512,512]{1,0:T(8,128)} async-done(((f32[512,2048]{1,0:T(8,128)}), f32[512,512]{1,0:T(8,128)}) %reduce-scatter.16.cloned.1.call-update) | async-done | bytes 1048592 | tf_op jit(solution)/shard_map/reduce_scatter | solution.py:395
  1182.5 283.2 %reduce-scatter.18.cloned.1.call-done = f32[512,2048]{1,0:T(8,128)} async-done(((f32[2048,2048]{1,0:T(8,128)}), f32[512,2048]{1,0:T(8,128)}) %reduce-scatter.18.cloned.1.call-update) | async-done | bytes 4194320 | tf_op jit(solution)/shard_map/reduce_scatter | solution.py:396
  1465.7 283.5 %reduce-scatter.20.cloned.1.call-done = f32[2048,512]{0,1:T(8,128)} async-done(((f32[2048,2048]{0,1:T(8,128)}), f32[2048,512]{0,1:T(8,128)}) %reduce-scatter.20.cloned.1.call-update) | async-done | bytes 4194320 | tf_op jit(solution)/shard_map/reduce_scatter | solution.py:397
  1749.1 214.7 %reduce-scatter.14.cloned.1.call-done = f32[512,1536]{1,0:T(8,128)} async-done(((f32[2048,1536]{1,0:T(8,128)}), f32[512,1536]{1,0:T(8,128)}) %reduce-scatter.14.cloned.1.call-update) | async-done | bytes 3145744 | tf_op jit(solution)/shard_map/reduce_scatter | solution.py:394
  1969.4 286.2 %all-reduce.27.cloned.1.call-done = (f32[512,1536]{1,0:T(8,128)}, f32[512,512]{1,0:T(8,128)}, f32[512,2048]{1,0:T(8,128)}, f32[2048,512]{0,1:T(8,128)}) async-done(((f32[512,1536]{1,0:T(8,128)}, f32[512,512]{1,0:T(8,128)}, f32[512,2048]{1,0:T(8,128)}, f32[2048,512]{0,1:T(8,128)}), (f32[512,1536]{1,0:T(8,128)}, f32[512,512]{1,0:T(8,128)}, f32[512,2048]{1,0:T(8,128)}, ...) | async-done | bytes 12582928 | tf_op jit(solution)/shard_map/psum | solution.py:399
  2260.0 7.9 fusion.176
  2269.1 8.3 fusion.171
  2287.6 85.6 %all-reduce.25.cloned.1.call-done = (f32[512,512]{1,0:T(8,128)}, f32[512,512]{1,0:T(8,128)}, f32[512,512]{1,0:T(8,128)}, f32[512,512]{1,0:T(8,128)}) async-done(((f32[512,512]{1,0:T(8,128)}, f32[512,512]{1,0:T(8,128)}, f32[512,512]{1,0:T(8,128)}, f32[512,512]{1,0:T(8,128)}), (f32[512,512]{1,0:T(8,128)}, f32[512,512]{1,0:T(8,128)}, f32[512,512]{1,0:T(8,128)}, ...) | async-done | bytes 4194320 | tf_op jit(solution)/shard_map/psum | solution.py:431
  2381.0 10.9 bitcast_add_fusion.5
  2391.9 7.9 fusion.177
  2403.1 9.8 multiply_add_fusion.8
  2452.5 14.9 fusion.157
  2467.4 70.9 %all-reduce.23.cloned.1.call-done = (f32[512,512]{1,0:T(8,128)}, f32[512,512]{1,0:T(8,128)}, f32[512,512]{1,0:T(8,128)}, f32[512,512]{1,0:T(8,128)}) async-done(((f32[512,512]{1,0:T(8,128)}, f32[512,512]{1,0:T(8,128)}, f32[512,512]{1,0:T(8,128)}, f32[512,512]{1,0:T(8,128)}), (f32[512,512]{1,0:T(8,128)}, f32[512,512]{1,0:T(8,128)}, f32[512,512]{1,0:T(8,128)}, ...) | async-done | bytes 4194320 | tf_op jit(solution)/shard_map/psum | solution.py:431
  2542.2 11.5 multiply_add_fusion.3
  2553.8 7.9 fusion.178
  2570.9 7.9 fusion.173
  2606.6 13.1 convolution_add_fusion.2
  2619.8 15.7 fusion.140
  2641.7 50.6 %all-reduce.21.cloned.1.call-done = (f32[512,512]{1,0:T(8,128)}, f32[512,512]{1,0:T(8,128)}, f32[512,512]{1,0:T(8,128)}, f32[512,512]{1,0:T(8,128)}) async-done(((f32[512,512]{1,0:T(8,128)}, f32[512,512]{1,0:T(8,128)}, f32[512,512]{1,0:T(8,128)}, f32[512,512]{1,0:T(8,128)}), (f32[512,512]{1,0:T(8,128)}, f32[512,512]{1,0:T(8,128)}, f32[512,512]{1,0:T(8,128)}, ...) | async-done | bytes 4194320 | tf_op jit(solution)/shard_map/psum | solution.py:431
  2739.2 8.3 fusion.174
  2747.5 8.3 fusion.138
  2770.7 69.5 %reduce-scatter.8.cloned.1.call-done = f32[256,2048]{1,0:T(8,128)} async-done(((f32[1024,2048]{1,0:T(8,128)}), f32[256,2048]{1,0:T(8,128)}) %reduce-scatter.8.cloned.1.call-update) | async-done | bytes 2097168 | tf_op jit(solution)/shard_map/reduce_scatter | solution.py:272
  2850.2 79.3 %all-reduce.19.cloned.1.call-done = (f32[512,512]{1,0:T(8,128)}, f32[512,512]{1,0:T(8,128)}, f32[512,512]{1,0:T(8,128)}, f32[512,512]{1,0:T(8,128)}) async-done(((f32[512,512]{1,0:T(8,128)}, f32[512,512]{1,0:T(8,128)}, f32[512,512]{1,0:T(8,128)}, f32[512,512]{1,0:T(8,128)}), (f32[512,512]{1,0:T(8,128)}, f32[512,512]{1,0:T(8,128)}, f32[512,512]{1,0:T(8,128)}, ...) | async-done | bytes 4194320 | tf_op jit(solution)/shard_map/psum | solution.py:431
  2933.4 11.2 fusion.137
  2953.5 8.3 fusion.175
  2982.4 17.4 fusion.75
  3016.7 45.3 %all-reduce.15.cloned.1.call-done = (f32[2048]{0:T(1024)}, f32[2048]{0:T(1024)}, f32[6144]{0:T(1024)}, f32[2048]{0:T(1024)}, f32[8192]{0:T(1024)}) async-done(((f32[2048]{0:T(1024)}, f32[2048]{0:T(1024)}, f32[6144]{0:T(1024)}, f32[2048]{0:T(1024)}, f32[8192]{0:T(1024)}), (f32[2048]{0:T(1024)}, f32[2048]{0:T(1024)}, f32[6144]{0:T(1024)}, f32[2048]{0:T(1024)}, f32[8192]{0:T(1024)})) %all-reduce.15.cloned.1.call-update) | async-done | bytes 81936 | tf_op jit(solution)/shard_map/psum | solution.py:415
  3084.6 67.6 %all-reduce.17.cloned.1.call-done = (f32[512,512]{1,0:T(8,128)}, f32[512,512]{1,0:T(8,128)}, f32[512,512]{1,0:T(8,128)}, f32[512,512]{1,0:T(8,128)}) async-done(((f32[512,512]{1,0:T(8,128)}, f32[512,512]{1,0:T(8,128)}, f32[512,512]{1,0:T(8,128)}, f32[512,512]{1,0:T(8,128)}), (f32[512,512]{1,0:T(8,128)}, f32[512,512]{1,0:T(8,128)}, f32[512,512]{1,0:T(8,128)}, ...) | async-done | bytes 4194320 | tf_op jit(solution)/shard_map/psum | solution.py:431
  3156.1 24.1 fusion.153
  3191.7 13.9 fusion.152
  3217.7 11.2 fusion.150
  (532 shorter events, 457.0 us)
Async XLA Ops:
  7.2 74.2 %all-gather.8.cloned.1.call-start = ((), (), s32[]{:S(2)}) async-start(), calls=%async_computation.11 | async-start | bytes 5242880 | tf_op jit(solution)/shard_map/all_gather | solution.py:160
  10.9 33.9 %copy-start.77 = (f32[2048]{0:T(1024)S(1)}, f32[2048]{0:T(1024)}, u32[]{:S(2)}) copy-start(f32[2048]{0:T(1024)} %param.52) | copy-start | bytes 24580
  10.9 33.8 %copy-start.83 = (f32[2048]{0:T(1024)S(1)}, f32[2048]{0:T(1024)}, u32[]{:S(2)}) copy-start(f32[2048]{0:T(1024)} %param.53) | copy-start | bytes 24580
  46.3 151.2 %all-gather.10.cloned.1.call-start = ((), (), s32[]{:S(2)}) async-start(), calls=%async_computation.12 | async-start | bytes 7864320 | tf_op jit(solution)/shard_map/all_gather | solution.py:168
  49.7 193.9 %all-gather.14.cloned.1.call-start = ((), (), s32[]{:S(2)}) async-start(), calls=%async_computation.14 | async-start | bytes 2621440 | tf_op jit(solution)/shard_map/all_gather | solution.py:169
  50.6 29.6 copy-start.115
  50.6 146.9 %copy-start.100 = (f32[1536]{0:T(1024)S(1)}, f32[1536]{0:T(1024)}, u32[]{:S(2)}) copy-start(f32[1536]{0:T(1024)} %param.55) | copy-start | bytes 18436
  50.6 227.6 %all-gather.20.cloned.1.call-start = ((), (), s32[]{:S(2)}) async-start(), calls=%async_computation.18 | async-start | bytes 5242880 | tf_op jit(solution)/shard_map/all_gather | solution.py:161
  80.2 349.7 %all-gather.12.cloned.1.call-start = ((), (), s32[]{:S(2)}) async-start(), calls=%async_computation.13 | async-start | bytes 10485760 | tf_op jit(solution)/shard_map/all_gather | solution.py:210
  81.5 138.8 %copy-start.74 = (f32[1024,16]{0,1:T(8,128)}, f32[1024,16]{0,1:T(8,128)S(1)}, u32[]{:S(2)}) copy-start(f32[1024,16]{0,1:T(8,128)S(1)} %get-tuple-element.1924) | copy-start | bytes 196612
  222.9 498.2 %all-gather.16.cloned.1.call-start = ((), (), s32[]{:S(2)}) async-start(), calls=%async_computation.15 | async-start | bytes 10485760 | tf_op jit(solution)/shard_map/all_gather | solution.py:170
  226.8 508.8 %all-gather.18.cloned.1.call-start = ((), (), s32[]{:S(2)}) async-start(), calls=%async_computation.16 | async-start | bytes 10485760 | tf_op jit(solution)/shard_map/all_gather | solution.py:171
  230.7 871.4 %reduce-scatter.10.cloned.1.call-start = ((), (), s32[]{:S(2)}) async-start(), calls=%async_computation.19 | async-start | bytes 20971520 | tf_op jit(solution)/shard_map/reduce_scatter | solution.py:361
  548.0 15.5 copy-start.29
  681.0 501.5 %reduce-scatter.16.cloned.1.call-start = ((), (), s32[]{:S(2)}) async-start(), calls=%async_computation.22 | async-start | bytes 5242880 | tf_op jit(solution)/shard_map/reduce_scatter | solution.py:395
  721.0 14.6 copy-start.104
  721.0 744.6 %reduce-scatter.18.cloned.1.call-start = ((), (), s32[]{:S(2)}) async-start(), calls=%async_computation.23 | async-start | bytes 20971520 | tf_op jit(solution)/shard_map/reduce_scatter | solution.py:396
  735.6 21.4 copy-start.113
  768.9 980.3 %reduce-scatter.20.cloned.1.call-start = ((), (), s32[]{:S(2)}) async-start(), calls=%async_computation.24 | async-start | bytes 20971520 | tf_op jit(solution)/shard_map/reduce_scatter | solution.py:397
  786.2 1177.6 %reduce-scatter.14.cloned.1.call-start = ((), (), s32[]{:S(2)}) async-start(), calls=%async_computation.21 | async-start | bytes 15728640 | tf_op jit(solution)/shard_map/reduce_scatter | solution.py:394
  1128.4 1127.2 %all-reduce.27.cloned.1.call-start = ((), (), s32[]{:S(2)}) async-start(), calls=%async_computation.31 | async-start | bytes 25165824 | tf_op jit(solution)/shard_map/psum | solution.py:399
  1963.9 409.4 %all-reduce.25.cloned.1.call-start = ((), (), s32[]{:S(2)}) async-start(), calls=%async_computation.30 | async-start | bytes 8388608 | tf_op jit(solution)/shard_map/psum | solution.py:431
  2284.5 302.0 %copy-start.28 = (f32[512,512]{1,0:T(8,128)}, f32[512,512]{1,0:T(8,128)S(1)}, u32[]{:S(2)}) copy-start(f32[512,512]{1,0:T(8,128)S(1)} %multiply_add_fusion.16) | copy-start | bytes 3145732
  2287.6 250.7 %all-reduce.23.cloned.1.call-start = ((), (), s32[]{:S(2)}) async-start(), calls=%async_computation.29 | async-start | bytes 8388608 | tf_op jit(solution)/shard_map/psum | solution.py:431
  2376.1 205.0 %copy-start.34 = (f32[512,512]{1,0:T(8,128)}, f32[512,512]{1,0:T(8,128)S(1)}, u32[]{:S(2)}) copy-start(f32[512,512]{1,0:T(8,128)S(1)} %multiply_multiply_fusion.2) | copy-start | bytes 3145732
  2452.5 239.8 %all-reduce.21.cloned.1.call-start = ((), (), s32[]{:S(2)}) async-start(), calls=%async_computation.28 | async-start | bytes 8388608 | tf_op jit(solution)/shard_map/psum | solution.py:431
  2606.5 159.8 %reduce-scatter.12.cloned.1.call-start = ((), (), s32[]{:S(2)}) async-start(), calls=%async_computation.20 | async-start | bytes 10485760 | tf_op jit(solution)/shard_map/reduce_scatter | solution.py:370
  2619.7 15.8 copy-start.47
  2619.7 220.4 %reduce-scatter.8.cloned.1.call-start = ((), (), s32[]{:S(2)}) async-start(), calls=%async_computation.17 | async-start | bytes 10485760 | tf_op jit(solution)/shard_map/reduce_scatter | solution.py:272
  2619.8 15.7 copy-start.72
  2641.3 288.2 %all-reduce.19.cloned.1.call-start = ((), (), s32[]{:S(2)}) async-start(), calls=%async_computation.27 | async-start | bytes 8388608 | tf_op jit(solution)/shard_map/psum | solution.py:431
  2730.0 17.4 copy-start.7
  2755.8 13.4 copy-start.94
  2755.9 84.3 %copy-start.85 = (f32[2048]{0:T(1024)S(1)}, f32[2048]{0:T(1024)}, u32[]{:S(2)}) copy-start(f32[2048]{0:T(1024)} %param.61) | copy-start | bytes 24580
  2755.9 84.3 %copy-start.86 = (f32[2048]{0:T(1024)S(1)}, f32[2048]{0:T(1024)}, u32[]{:S(2)}) copy-start(f32[2048]{0:T(1024)} %param.57) | copy-start | bytes 24580
  2758.2 86.7 %copy-start.79 = (f32[8192]{0:T(1024)}, f32[8192]{0:T(1024)S(1)}, u32[]{:S(2)}) copy-start(f32[8192]{0:T(1024)S(1)} %dynamic_update_slice.17) | copy-start | bytes 98308
  2758.6 86.4 %copy-start.80 = (f32[6144]{0:T(1024)}, f32[6144]{0:T(1024)S(1)}, u32[]{:S(2)}) copy-start(f32[6144]{0:T(1024)S(1)} %dynamic_update_slice.16) | copy-start | bytes 73732
  2845.0 157.9 %all-to-all-start.3 = ((bf16[4,64,2048]{2,1,0:T(8,128)(2,1)}), bf16[4,64,2048]{2,1,0:T(8,128)(2,1)S(1)}, u32[]{:S(2)}, u32[]{:S(2)}) async-start(bf16[4,64,2048]{2,1,0:T(8,128)(2,1)} %bitcast.384), calls=%async_computation.6 | async-start | bytes 2097152 | tf_op jit(solution)/shard_map/all_to_all | solution.py:381
  2849.6 212.4 %all-reduce.15.cloned.1.call-start = ((), (), s32[]{:S(2)}) async-start(), calls=%async_computation.25 | async-start | bytes 163840 | tf_op jit(solution)/shard_map/psum | solution.py:415
  2850.1 302.1 %all-reduce.17.cloned.1.call-start = ((), (), s32[]{:S(2)}) async-start(), calls=%async_computation.26 | async-start | bytes 8388608 | tf_op jit(solution)/shard_map/psum | solution.py:431
  2981.1 18.7 copy-start.40
  2982.4 17.4 copy-start.42
  3002.8 68.3 %all-to-all-start.1 = ((bf16[4,64,2048]{2,1,0:T(8,128)(2,1)}), bf16[4,64,2048]{2,1,0:T(8,128)(2,1)S(1)}, u32[]{:S(2)}, u32[]{:S(2)}) async-start(bf16[4,64,2048]{2,1,0:T(8,128)(2,1)} %bitcast.383), calls=%async_computation.2 | async-start | bytes 2097152 | tf_op jit(solution)/shard_map/all_to_all | solution.py:380
  3007.8 54.2 %copy-start.101 = (f32[1536]{0:T(1024)S(1)}, f32[1536]{0:T(1024)}, u32[]{:S(2)}) copy-start(f32[1536]{0:T(1024)} %param.55) | copy-start | bytes 18436
  3007.9 54.2 %copy-start.102 = (f32[1536]{0:T(1024)S(1)}, f32[1536]{0:T(1024)}, u32[]{:S(2)}) copy-start(f32[1536]{0:T(1024)} %param.70) | copy-start | bytes 18436
  3007.9 54.2 %copy-start.103 = (f32[1536]{0:T(1024)S(1)}, f32[1536]{0:T(1024)}, u32[]{:S(2)}) copy-start(f32[1536]{0:T(1024)} %param.71) | copy-start | bytes 18436
  3007.9 55.5 %copy-start.105 = (f32[2048]{0:T(1024)S(1)}, f32[2048]{0:T(1024)}, u32[]{:S(2)}) copy-start(f32[2048]{0:T(1024)} %param.74) | copy-start | bytes 24580
  3007.9 55.5 %copy-start.106 = (f32[2048]{0:T(1024)S(1)}, f32[2048]{0:T(1024)}, u32[]{:S(2)}) copy-start(f32[2048]{0:T(1024)} %param.75) | copy-start | bytes 24580
  3007.9 56.9 %copy-start.95 = (f32[2048]{0:T(1024)S(1)}, f32[2048]{0:T(1024)}, u32[]{:S(2)}) copy-start(f32[2048]{0:T(1024)} %param.66) | copy-start | bytes 24580
  3007.9 56.8 %copy-start.96 = (f32[2048]{0:T(1024)S(1)}, f32[2048]{0:T(1024)}, u32[]{:S(2)}) copy-start(f32[2048]{0:T(1024)} %param.67) | copy-start | bytes 24580
  3007.9 58.2 %copy-start.84 = (f32[2048]{0:T(1024)S(1)}, f32[2048]{0:T(1024)}, u32[]{:S(2)}) copy-start(f32[2048]{0:T(1024)} %param.53) | copy-start | bytes 24580
  3007.9 58.1 %copy-start.97 = (f32[2048]{0:T(1024)S(1)}, f32[2048]{0:T(1024)}, u32[]{:S(2)}) copy-start(f32[2048]{0:T(1024)} %param.68) | copy-start | bytes 24580
  3008.0 58.1 %copy-start.98 = (f32[2048]{0:T(1024)S(1)}, f32[2048]{0:T(1024)}, u32[]{:S(2)}) copy-start(f32[2048]{0:T(1024)} %param.69) | copy-start | bytes 24580
  3008.0 59.5 %copy-start.107 = (f32[2048]{0:T(1024)S(1)}, f32[2048]{0:T(1024)}, u32[]{:S(2)}) copy-start(f32[2048]{0:T(1024)} %param.76) | copy-start | bytes 24580
  3008.0 59.4 %copy-start.108 = (f32[2048]{0:T(1024)S(1)}, f32[2048]{0:T(1024)}, u32[]{:S(2)}) copy-start(f32[2048]{0:T(1024)} %param.77) | copy-start | bytes 24580
  3008.0 59.4 %copy-start.109 = (f32[2048]{0:T(1024)S(1)}, f32[2048]{0:T(1024)}, u32[]{:S(2)}) copy-start(f32[2048]{0:T(1024)} %param.73) | copy-start | bytes 24580
  3008.0 59.4 %copy-start.110 = (f32[2048]{0:T(1024)S(1)}, f32[2048]{0:T(1024)}, u32[]{:S(2)}) copy-start(f32[2048]{0:T(1024)} %param.72) | copy-start | bytes 24580
  3191.6 14.0 copy-start.54
  3191.6 15.9 copy-start.39
  3191.6 15.9 copy-start.41
  3191.6 15.9 copy-start.43
  3191.7 15.9 copy-start.44
  3191.7 15.9 copy-start.45
  3191.7 15.9 copy-start.69
  (77 other events, 477.3 us)
Sparse Core Ops, SparseCore 0:
  46.4 33.5 all-gather.7
  82.1 115.3 all-gather.9
  199.6 43.8 all-gather.13
  244.9 33.2 all-gather.19
  280.2 149.5 all-gather.11
  431.9 147.7 all-gather.15
  581.8 147.7 all-gather.17
  732.0 370.0 reduce-scatter.9
  1105.0 77.4 reduce-scatter.15
  1184.7 280.9 reduce-scatter.17
  1468.0 281.0 reduce-scatter.19
  1751.3 212.4 reduce-scatter.13
  1966.5 289.1 all-reduce.26
  2287.7 85.5 all-reduce.24
  2452.6 85.6 all-reduce.22
  2606.6 85.6 all-reduce.20
  2694.8 71.4 reduce-scatter.11
  2768.7 71.3 reduce-scatter.7
  2843.9 85.5 all-reduce.18
  2937.4 124.5 all-reduce.14
  3065.2 87.0 all-reduce.16
where the time goes:
time: 3260 us; the launch traced here: 3240 us
  waiting for transfers between devices  2220 us (68%)
  matrix products  622 us (19%)
  local copies, waits for them, and re-layouts  193 us (6%)
  other arithmetic  84.8 us (3%)
  blocking collectives  59.9 us (2%)
  loops' own time  32.6 us (1%)
    psum x5, waiting for transfers between devices, per_device(): lax.psum((local_gram(current[0]), local_gram(current[1]), local_gram(curr...  354 us
    reduce_scatter x1, waiting for transfers between devices, per_device(): lax.psum_scatter(key_extras.reshape(pack_rows, 2, head_cols), 'fsdp', sca...  314 us
    psum x1, waiting for transfers between devices, per_device(): lax.psum((shards[0], shards[1], shards[2], shards[3]), 'rep')  286 us
    reduce_scatter x1, waiting for transfers between devices, per_device(): lax.psum_scatter(reduce_term, 'fsdp', scatter_dimension=1, tiled=True)  283 us
    reduce_scatter x1, waiting for transfers between devices, per_device(): lax.psum_scatter(expand_term, 'fsdp', scatter_dimension=0, tiled=True)  283 us
    reduce_scatter x1, waiting for transfers between devices, per_device(): lax.psum_scatter(project_term, 'fsdp', scatter_dimension=0, tiled=True)  215 us
    dot_general x20, matrix products, schulz_turn(): jnp.dot(mixing, block_part, precision=lax.Precision.HIGHEST)  159 us
    all_gather x1, waiting for transfers between devices, per_device(): paired_group = lax.all_gather(paired_here, 'fsdp', axis=0, tiled=True)  144 us
  transfers between devices with their start and end apart: 23, of which 18 were waited for; matrix products, arithmetic and copies ran while one was open for 19% of the time, Pallas kernels for 0%

commit v1 on v0

--- a/solution.py
+++ b/solution.py
@@ -1,8 +1,11 @@
+import functools
 import math
 
 import jax
 import jax.numpy as jnp
 from jax import lax
+from jax.experimental import pallas as pl
+from jax.experimental.pallas import tpu as pltpu
 from jax.sharding import PartitionSpec as P
 
 D = 2048
@@ -96,7 +99,349 @@
     return (param_new, moment_one, moment_two)
 
 
-def per_device(
+BLOCK = 256
+LANES = 128
+
+
+def dot_nt(left, right):
+    return lax.dot_general(
+        left, right, (((1,), (1,)), ((), ())), preferred_element_type=jnp.float32
+    )
+
+
+def dot_nn(left, right):
+    return lax.dot_general(
+        left, right, (((1,), (0,)), ((), ())), preferred_element_type=jnp.float32
+    )
+
+
+def turn_pairs(values, cosine, sine):
+    lane = lax.broadcasted_iota(jnp.int32, values.shape, 1) % HEAD_DIM
+    width = values.shape[1]
+    ahead = pltpu.roll(values, width - ROT // 2, 1)
+    behind = pltpu.roll(values, ROT // 2, 1)
+    return values * cosine + jnp.where(lane < ROT // 2, ahead, behind) * sine
+
+
+def rope_body(joined_ref, cosine_ref, sine_ref, q_ref, k_ref, v_ref, kt_ref, vt_ref):
+    rows = joined_ref[...].reshape(BLOCK, 3 * LANES)
+    cosine, sine = cosine_ref[...], sine_ref[...]
+    queries = turn_pairs(rows[:, :LANES], cosine, sine).astype(jnp.bfloat16)
+    q_ref[...] = queries * jnp.bfloat16(HEAD_DIM**-0.5)
+    keys = turn_pairs(rows[:, LANES : 2 * LANES], cosine, sine)
+    k_ref[...] = keys.astype(jnp.bfloat16)
+    kt_ref[...] = keys.T.astype(jnp.bfloat16)
+    values = rows[:, 2 * LANES :]
+    v_ref[...] = values.astype(jnp.bfloat16)
+    vt_ref[...] = values.T.astype(jnp.bfloat16)
+
+
+def unrope_body(dq_ref, dk_ref, dv_ref, cosine_ref, sine_ref, out_ref, sum_ref):
+    cosine, sine = cosine_ref[...], -sine_ref[...]
+    parts = (
+        turn_pairs(dq_ref[...], cosine, sine),
+        turn_pairs(dk_ref[...], cosine, sine),
+        dv_ref[...],
+    )
+
+    @pl.when((pl.program_id(0) == 0) & (pl.program_id(1) == 0))
+    def _():
+        sum_ref[...] = jnp.zeros_like(sum_ref)
+
+    for part_at, part in enumerate(parts):
+        low = part.astype(jnp.bfloat16)
+        cols = slice(part_at * LANES, (part_at + 1) * LANES)
+        out_ref[..., cols] = low.reshape(out_ref.shape[:-1] + (LANES,))
+        wide = low.astype(jnp.float32).reshape(BLOCK // 8, 8, LANES)
+        sum_ref[:, cols] += jnp.sum(wide, axis=0)
+
+
+def sequence_starts(lengths_ref, row_ids):
+    offset = jnp.int32(0)
+    starts = jnp.zeros_like(row_ids)
+    for seq_at in range(lengths_ref.shape[0] - 1):
+        offset = offset + lengths_ref[seq_at]
+        starts = jnp.where(row_ids >= offset, offset, starts)
+    return starts
+
+
+def first_block(lengths_ref, block_at):
+    row = block_at * BLOCK
+    offset = jnp.int32(0)
+    start = jnp.int32(0)
+    for seq_at in range(lengths_ref.shape[0] - 1):
+        offset = offset + lengths_ref[seq_at]
+        start = jnp.where(row >= offset, offset, start)
+    return start // BLOCK
+
+
+def head_lanes(values, head):
+    lane = lax.broadcasted_iota(jnp.int32, values.shape, 1)
+    return jnp.where(lane // HEAD_DIM == head, values, jnp.zeros_like(values))
+
+
+def masked_scores(key_ref, queries, key_block, query_ids, starts):
+    first = pl.multiple_of(key_block * BLOCK, BLOCK)
+    scores = dot_nt(key_ref[pl.ds(first, BLOCK), :], queries)
+    key_ids = first + lax.broadcasted_iota(jnp.int32, (BLOCK, BLOCK), 0)
+    allowed = (key_ids >= starts) & (key_ids <= query_ids)
+    return jnp.where(allowed, scores, NEG_LARGE)
+
+
+def attend_body(lengths_ref, q_ref, k_ref, vt_ref, out_ref, stat_ref, held):
+    block_at = pl.program_id(0) * pl.num_programs(1) + pl.program_id(1)
+    begin = first_block(lengths_ref, block_at)
+    query_ids = block_at * BLOCK + lax.broadcasted_iota(jnp.int32, (1, BLOCK), 1)
+    starts = sequence_starts(lengths_ref, query_ids)
+    queries = q_ref[...]
+    outs = []
+    for head in range(LANES // HEAD_DIM):
+        one = head_lanes(queries, head)
+
+        def score_step(key_block, top):
+            scores = masked_scores(k_ref, one, key_block, query_ids, starts)
+            held[key_block] = scores
+            return jnp.maximum(top, jnp.max(scores, axis=0, keepdims=True))
+
+        top = lax.fori_loop(
+            begin, block_at + 1, score_step, jnp.full((1, BLOCK), NEG_LARGE, jnp.float32)
+        )
+
+        def total_step(key_block, total):
+            raised = jnp.exp(held[key_block] - top)
+            held[key_block] = raised
+            return total + jnp.sum(raised, axis=0, keepdims=True)
+
+        total = lax.fori_loop(
+            begin, block_at + 1, total_step, jnp.zeros((1, BLOCK), jnp.float32)
+        )
+        inverse = 1.0 / total
+
+        def value_step(key_block, accum):
+            first = pl.multiple_of(key_block * BLOCK, BLOCK)
+            probs_low = (held[key_block] * inverse).astype(jnp.bfloat16)
+            return accum + dot_nn(vt_ref[:, pl.ds(first, BLOCK)], probs_low)
+
+        accum = lax.fori_loop(
+            begin, block_at + 1, value_step, jnp.zeros((LANES, BLOCK), jnp.float32)
+        )
+        outs.append(accum)
+        stat_ref[pl.ds(head, 1), :] = top + jnp.log(total)
+    row = lax.broadcasted_iota(jnp.int32, (LANES, BLOCK), 0)
+    merged = jnp.where(row < HEAD_DIM, outs[0], outs[1])
+    out_ref[...] = merged.T.astype(jnp.bfloat16).reshape(out_ref.shape)
+
+
+def attend_back_body(
+    lengths_ref,
+    q_ref,
+    grad_ref,
+    stat_ref,
+    k_ref,
+    v_ref,
+    kt_ref,
+    dq_ref,
+    dk_ref,
+    dv_ref,
+    held_probs,
+    held_grads,
+):
+    block_at = pl.program_id(0) * pl.num_programs(1) + pl.program_id(1)
+
+    @pl.when(block_at == 0)
+    def _():
+        dk_ref[...] = jnp.zeros_like(dk_ref)
+        dv_ref[...] = jnp.zeros_like(dv_ref)
+
+    begin = first_block(lengths_ref, block_at)
+    query_ids = block_at * BLOCK + lax.broadcasted_iota(jnp.int32, (1, BLOCK), 1)
+    starts = sequence_starts(lengths_ref, query_ids)
+    queries = q_ref[...]
+    grads = grad_ref[...].reshape(BLOCK, LANES)
+    outs = []
+    for head in range(LANES // HEAD_DIM):
+        one = head_lanes(queries, head)
+        one_grad = head_lanes(grads, head)
+        log_total = stat_ref[pl.ds(head, 1), :]
+
+        def probs_step(key_block, delta):
+            first = pl.multiple_of(key_block * BLOCK, BLOCK)
+            scores = masked_scores(k_ref, one, key_block, query_ids, starts)
+            probs = jnp.exp(scores - log_total)
+            d_probs = dot_nt(v_ref[pl.ds(first, BLOCK), :], one_grad)
+            held_probs[key_block] = probs
+            held_grads[key_block] = d_probs
+            return delta + jnp.sum(probs * d_probs, axis=0, keepdims=True)
+
+        delta = lax.fori_loop(
+            begin, block_at + 1, probs_step, jnp.zeros((1, BLOCK), jnp.float32)
+        )
+
+        def grads_step(key_block, accum):
+            first = pl.multiple_of(key_block * BLOCK, BLOCK)
+            rows = pl.ds(first, BLOCK)
+            probs = held_probs[key_block]
+            d_scores = (probs * (held_grads[key_block] - delta)).astype(jnp.bfloat16)
+            dk_ref[rows, :] += dot_nn(d_scores, one)
+            dv_ref[rows, :] += dot_nn(probs.astype(jnp.bfloat16), one_grad)
+            return accum + dot_nn(kt_ref[:, rows], d_scores)
+
+        outs.append(
+            lax.fori_loop(
+                begin, block_at + 1, grads_step, jnp.zeros((LANES, BLOCK), jnp.float32)
+            )
+        )
+    row = lax.broadcasted_iota(jnp.int32, (LANES, BLOCK), 0)
+    merged = jnp.where(row < HEAD_DIM, outs[0], outs[1])
+    dq_ref[...] = merged.T * HEAD_DIM**-0.5
+
+
+def given_block(dealt, groups, slot, width):
+    return pl.BlockSpec((dealt, 1, 1, slot, width), lambda d, n, *_: (0, n, d, 0, 0))
+
+
+def rope(joined, cosine, sine, dealt, groups):
+    rows = joined.shape[0]
+    slot = rows // (dealt * groups * dealt)
+    view = joined.reshape(dealt, groups, dealt, slot, 3 * LANES)
+    flat = pl.BlockSpec((BLOCK, LANES), lambda d, n: (d * groups + n, 0))
+    turned = pl.BlockSpec((LANES, BLOCK), lambda d, n: (0, d * groups + n))
+    straight = jax.ShapeDtypeStruct((rows, LANES), jnp.bfloat16)
+    across = jax.ShapeDtypeStruct((LANES, rows), jnp.bfloat16)
+    return pl.pallas_call(
+        rope_body,
+        grid=(dealt, groups),
+        in_specs=[given_block(dealt, groups, slot, 3 * LANES), flat, flat],
+        out_specs=[flat, flat, flat, turned, turned],
+        out_shape=[straight, straight, straight, across, across],
+        cost_estimate=pl.CostEstimate(
+            flops=rows * LANES * 12, bytes_accessed=rows * LANES * 30, transcendentals=0
+        ),
+        name="rope",
+    )(view, cosine, sine)
+
+
+def unrope(d_queries, d_keys, d_values, cosine, sine, dealt, groups):
+    rows = d_queries.shape[0]
+    slot = rows // (dealt * groups * dealt)
+    flat = pl.BlockSpec((BLOCK, LANES), lambda d, n: (d * groups + n, 0))
+    out, sums = pl.pallas_call(
+        unrope_body,
+        grid=(dealt, groups),
+        in_specs=[flat] * 5,
+        out_specs=[
+            given_block(dealt, groups, slot, 3 * LANES),
+            pl.BlockSpec((8, 3 * LANES), lambda d, n: (0, 0)),
+        ],
+        out_shape=[
+            jax.ShapeDtypeStruct((dealt, groups, dealt, slot, 3 * LANES), jnp.bfloat16),
+            jax.ShapeDtypeStruct((8, 3 * LANES), jnp.float32),
+        ],
+        cost_estimate=pl.CostEstimate(
+            flops=rows * LANES * 12, bytes_accessed=rows * LANES * 26, transcendentals=0
+        ),
+        name="unrope",
+    )(d_queries, d_keys, d_values, cosine, sine)
+    return out.reshape(rows, 3 * LANES), jnp.sum(sums, axis=0)
+
+
+def attend(row_lengths, queries, keys, values_turned, dealt, groups):
+    rows = queries.shape[0]
+    slot = rows // (dealt * groups * dealt)
+    flat = pl.BlockSpec((BLOCK, LANES), lambda d, n, _: (d * groups + n, 0))
+    attended, stats = pl.pallas_call(
+        attend_body,
+        grid_spec=pltpu.PrefetchScalarGridSpec(
+            num_scalar_prefetch=1,
+            grid=(dealt, groups),
+            in_specs=[
+                flat,
+                pl.BlockSpec((rows, LANES), lambda d, n, _: (0, 0)),
+                pl.BlockSpec((LANES, rows), lambda d, n, _: (0, 0)),
+            ],
+            out_specs=[
+                given_block(dealt, groups, slot, LANES),
+                pl.BlockSpec((8, BLOCK), lambda d, n, _: (0, d * groups + n)),
+            ],
+            scratch_shapes=[pltpu.VMEM((rows // BLOCK, BLOCK, BLOCK), jnp.float32)],
+        ),
+        out_shape=[
+            jax.ShapeDtypeStruct((dealt, groups, dealt, slot, LANES), jnp.bfloat16),
+            jax.ShapeDtypeStruct((8, rows), jnp.float32),
+        ],
+        cost_estimate=pl.CostEstimate(
+            flops=rows * rows * LANES * 2,
+            bytes_accessed=rows * LANES * 10,
+            transcendentals=rows * rows // 2,
+        ),
+        name="attend",
+    )(row_lengths, queries, keys, values_turned)
+    return attended.reshape(rows, LANES), stats
+
+
+def attend_back(row_lengths, queries, grads, stats, keys, values, keys_turned, dealt, groups):
+    rows = queries.shape[0]
+    slot = rows // (dealt * groups * dealt)
+    flat = pl.BlockSpec((BLOCK, LANES), lambda d, n, _: (d * groups + n, 0))
+    whole = pl.BlockSpec((rows, LANES), lambda d, n, _: (0, 0))
+    wide = jax.ShapeDtypeStruct((rows, LANES), jnp.float32)
+    return pl.pallas_call(
+        attend_back_body,
+        grid_spec=pltpu.PrefetchScalarGridSpec(
+            num_scalar_prefetch=1,
+            grid=(dealt, groups),
+            in_specs=[
+                flat,
+                given_block(dealt, groups, slot, LANES),
+                pl.BlockSpec((8, BLOCK), lambda d, n, _: (0, d * groups + n)),
+                whole,
+                whole,
+                pl.BlockSpec((LANES, rows), lambda d, n, _: (0, 0)),
+            ],
+            out_specs=[flat, whole, whole],
+            scratch_shapes=[pltpu.VMEM((rows // BLOCK, BLOCK, BLOCK), jnp.float32)] * 2,
+        ),
+        out_shape=[wide, wide, wide],
+        cost_estimate=pl.CostEstimate(
+            flops=rows * rows * LANES * 4,
+            bytes_accessed=rows * LANES * 24,
+            transcendentals=rows * rows // 2,
+        ),
+        name="attend_back",
+    )(
+        row_lengths,
+        queries,
+        grads.reshape(dealt, groups, dealt, slot, LANES),
+        stats,
+        keys,
+        values,
+        keys_turned,
+    )
+
+
+def gelu_slope(values_in):
+    scale = math.sqrt(2.0 / math.pi)
+    bent = jnp.tanh(scale * (values_in + 0.044715 * values_in * values_in * values_in))
+    return 0.5 * (1.0 + bent) + 0.5 * values_in * (1.0 - bent * bent) * scale * (
+        1.0 + 3.0 * 0.044715 * values_in * values_in
+    )
+
+
+def schulz_chain(gram):
+    precise = functools.partial(jnp.dot, precision=lax.Precision.HIGHEST)
+    eye = jnp.eye(gram.shape[0], dtype=jnp.float32)
+    chain = None
+    for turn_id in range(SCHULZ_STEPS):
+        turn = (
+            SCHULZ_FIRST * eye + SCHULZ_SECOND * gram + SCHULZ_THIRD * precise(gram, gram)
+        )
+        chain = turn if chain is None else precise(turn, chain)
+        if turn_id < SCHULZ_STEPS - 1:
+            gram = precise(precise(turn, gram), turn)
+    return chain
+
+
+def gathered_weights(
     tokens,
     cotangent,
     placement,
@@ -519,9 +864,295 @@
     )
 
 
+def per_device(axis_sizes, *arguments):
+    heads = arguments[8].shape[0] // (3 * HEAD_DIM)
+    shard_rows = arguments[0].shape[0]
+    dealt = axis_sizes["fsdp"]
+    fits = heads * HEAD_DIM == dealt * LANES and shard_rows == BLOCK and BLOCK % (8 * dealt) == 0
+    return (split_heads if fits else gathered_weights)(*arguments)
+
+
+def split_heads(
+    tokens,
+    cotangent,
+    placement,
+    lengths,
+    step_count,
+    norm_gain,
+    norm_bias,
+    project_weight,
+    project_bias,
+    output_weight,
+    output_bias,
+    expand_weight,
+    expand_bias,
+    reduce_weight,
+    reduce_bias,
+    project_momentum,
+    output_momentum,
+    expand_momentum,
+    reduce_momentum,
+    norm_gain_first,
+    norm_gain_second,
+    norm_bias_first,
+    norm_bias_second,
+    project_bias_first,
+    project_bias_second,
+    output_bias_first,
+    output_bias_second,
+    expand_bias_first,
+    expand_bias_second,
+    reduce_bias_first,
+    reduce_bias_second,
+):
+    dealt = lax.axis_size("fsdp")
+    groups = lax.axis_size("ns")
+    shard_rows = tokens.shape[0]
+    slot = shard_rows // dealt
+    pack_rows = shard_rows * dealt * groups
+    fsdp_at = lax.axis_index("fsdp")
+    ns_at = lax.axis_index("ns")
+    row_lengths = lengths[0]
+    low = jnp.bfloat16
+
+    within = placement % shard_rows
+    dest = placement // shard_rows // groups % dealt
+    slot_index = dest * slot + within - fsdp_at * slot
+    slots = jnp.arange(shard_rows, dtype=jnp.int32)
+    deal = (slot_index[None, :] == slots[:, None]).astype(low)
+    sorted_tokens = jnp.dot(deal, tokens, preferred_element_type=jnp.float32)
+    sorted_cotangent = jnp.dot(deal, cotangent, preferred_element_type=jnp.float32).astype(low)
+    normed, norm_back = jax.vjp(layer_norm, sorted_tokens, norm_gain, norm_bias)
+    normed_all = lax.all_gather(normed.astype(low), ("fsdp", "ns"), axis=0, tiled=True)
+    cotangent_all = lax.all_gather(sorted_cotangent, ("fsdp", "ns"), axis=0, tiled=True)
+
+    def exchange(pieces):
+        return lax.all_to_all(pieces, "fsdp", split_axis=0, concat_axis=0, tiled=True)
+
+    col = jnp.arange(3 * LANES, dtype=jnp.int32)
+    dest_col = (
+        col % (3 * HEAD_DIM) // HEAD_DIM * LANES
+        + col // (3 * HEAD_DIM) * HEAD_DIM
+        + col % HEAD_DIM
+    )
+    shuffle = (dest_col[:, None] == col[None, :]).astype(low)
+    width = project_weight.shape[0]
+    ff_here = expand_bias.shape[0] // dealt
+    project_pieces = jnp.einsum(
+        "rfc,cd->frd",
+        project_weight.astype(low).reshape(width, dealt, 3 * LANES),
+        shuffle,
+        preferred_element_type=low,
+    )
+    project_full = exchange(project_pieces).reshape(dealt * width, 3 * LANES)
+    expand_pieces = expand_weight.astype(low).reshape(width, dealt, ff_here).transpose(1, 0, 2)
+    expand_full = exchange(expand_pieces).reshape(dealt * width, ff_here)
+    output_pieces = output_weight.astype(low).reshape(dealt, LANES, width)
+    output_full = exchange(output_pieces).transpose(1, 0, 2).reshape(LANES, dealt * width)
+    reduce_pieces = reduce_weight.astype(low).reshape(dealt, ff_here, width)
+    reduce_full = exchange(reduce_pieces).transpose(1, 0, 2).reshape(ff_here, dealt * width)
+
+    pack_ids = jnp.arange(pack_rows, dtype=jnp.int32)
+    positions = pack_ids - sequence_layout(row_lengths, pack_ids)[1]
+    cosine_half, sine_half = rope_tables(positions)
+    still = jnp.zeros((pack_rows, HEAD_DIM - ROT), jnp.float32)
+    head_cosine = jnp.concatenate([cosine_half, cosine_half, still + 1.0], axis=1)
+    head_sine = jnp.concatenate([-sine_half, sine_half, still], axis=1)
+    cosine = jnp.concatenate([head_cosine, head_cosine], axis=1)
+    sine = jnp.concatenate([head_sine, head_sine], axis=1)
+
+    project_bias_here = lax.dynamic_slice_in_dim(project_bias, fsdp_at * 3 * LANES, 3 * LANES)
+    project_bias_here = (
+        project_bias_here.reshape(-1, 3, HEAD_DIM).transpose(1, 0, 2).reshape(3 * LANES)
+    )
+    expand_bias_here = lax.dynamic_slice_in_dim(expand_bias, fsdp_at * ff_here, ff_here)
+    joined = (
+        jnp.dot(normed_all, project_full, preferred_element_type=jnp.float32) + project_bias_here
+    )
+    queries, keys, values, keys_turned, values_turned = rope(joined, cosine, sine, dealt, groups)
+    attended_low, stats = attend(row_lengths, queries, keys, values_turned, dealt, groups)
+    hidden = jnp.dot(normed_all, expand_full, preferred_element_type=jnp.float32) + expand_bias_here
+    activated_low = gelu_tanh(hidden).astype(low)
+    branch = jnp.dot(attended_low, output_full, preferred_element_type=jnp.float32) + jnp.dot(
+        activated_low, reduce_full, preferred_element_type=jnp.float32
+    )
+    branch_sum = lax.psum_scatter(
+        branch.astype(low), ("fsdp", "ns"), scatter_dimension=0, tiled=True
+    ).astype(jnp.float32)
+    layer_rows = (sorted_tokens + branch_sum + output_bias + reduce_bias).astype(low)
+
+    d_attended = dot_nt(cotangent_all, output_full).astype(low)
+    d_hidden = (gelu_slope(hidden) * dot_nt(cotangent_all, reduce_full)).astype(low)
+    d_queries, d_keys, d_values = attend_back(
+        row_lengths, queries, d_attended, stats, keys, values, keys_turned, dealt, groups
+    )
+    d_joined, d_joined_sum = unrope(d_queries, d_keys, d_values, cosine, sine, dealt, groups)
+    d_normed_part = dot_nt(d_joined, project_full) + dot_nt(d_hidden, expand_full)
+    d_normed = lax.psum_scatter(
+        d_normed_part.astype(low), ("fsdp", "ns"), scatter_dimension=0, tiled=True
+    ).astype(jnp.float32)
+    d_tokens_norm, gain_term, shift_term = norm_back(d_normed)
+    input_rows = (sorted_cotangent.astype(jnp.float32) + d_tokens_norm).astype(low)
+
+    def undeal(rows):
+        return lax.dot_general(
+            deal, rows, (((0,), (0,)), ((), ())), preferred_element_type=jnp.float32
+        ).astype(low)
+
+    layer_output = undeal(layer_rows)
+    input_grad = undeal(input_rows)
+
+    def outer(left, right):
+        return lax.dot_general(
+            left, right, (((0,), (0,)), ((), ())), preferred_element_type=jnp.float32
+        ).astype(low)
+
+    def both_packs(shard):
+        twin = lax.ppermute(shard, "rep", [(0, 1), (1, 0)]) if lax.axis_size("rep") == 2 else None
+        if twin is None:
+            return lax.psum(shard.astype(jnp.float32), "rep")
+        return shard.astype(jnp.float32) + twin.astype(jnp.float32)
+
+    reduce_term = outer(activated_low, cotangent_all).reshape(ff_here, dealt, width)
+    reduce_grad = both_packs(
+        exchange(reduce_term.transpose(1, 0, 2)).reshape(dealt * ff_here, width)
+    )
+    output_term = outer(attended_low, cotangent_all).reshape(LANES, dealt, width)
+    output_grad = both_packs(
+        exchange(output_term.transpose(1, 0, 2)).reshape(dealt * LANES, width)
+    )
+    expand_term = outer(normed_all, d_hidden).reshape(dealt, width, ff_here)
+    expand_grad = both_packs(
+        exchange(expand_term).transpose(1, 0, 2).reshape(width, dealt * ff_here)
+    )
+    project_term = jnp.einsum(
+        "frd,cd->frc",
+        outer(normed_all, d_joined).reshape(dealt, width, 3 * LANES),
+        shuffle,
+        preferred_element_type=low,
+    )
+    project_grad = both_packs(
+        exchange(project_term).transpose(1, 0, 2).reshape(width, dealt * 3 * LANES)
+    )
+
+    part_at = ns_at * dealt + fsdp_at
+    project_bias_width = project_bias.shape[0]
+    expand_bias_width = expand_bias.shape[0]
+    project_bias_part = lax.dynamic_update_slice(
+        jnp.zeros((project_bias_width * groups,), jnp.float32),
+        d_joined_sum.reshape(3, -1, HEAD_DIM).transpose(1, 0, 2).reshape(3 * LANES),
+        (part_at * 3 * LANES,),
+    )
+    expand_bias_part = lax.dynamic_update_slice(
+        jnp.zeros((expand_bias_width * groups,), jnp.float32),
+        jnp.sum(d_hidden, axis=0, dtype=jnp.float32),
+        (part_at * ff_here,),
+    )
+    cotangent_sum = jnp.sum(sorted_cotangent, axis=0, dtype=jnp.float32)
+    gain_grad, shift_grad, cotangent_total, project_bias_all, expand_bias_all = lax.psum(
+        (gain_term, shift_term, cotangent_sum, project_bias_part, expand_bias_part),
+        ("rep", "fsdp", "ns"),
+    )
+    project_bias_grad = lax.dynamic_slice_in_dim(
+        project_bias_all, ns_at * project_bias_width, project_bias_width
+    )
+    expand_bias_grad = lax.dynamic_slice_in_dim(
+        expand_bias_all, ns_at * expand_bias_width, expand_bias_width
+    )
+
+    project_mom = MUON_DECAY * project_momentum + project_grad
+    output_mom = MUON_DECAY * output_momentum + output_grad
+    expand_mom = MUON_DECAY * expand_momentum + expand_grad
+    reduce_mom = MUON_DECAY * reduce_momentum + reduce_grad
+    precise = functools.partial(lax.dot_general, precision=lax.Precision.HIGHEST)
+    by_row = (((1,), (1,)), ((), ()))
+    by_col = (((0,), (0,)), ((), ()))
+    grams = jnp.stack(
+        [
+            precise(project_mom, project_mom, by_row),
+            precise(output_mom, output_mom, by_col),
+            precise(expand_mom, expand_mom, by_row),
+            precise(reduce_mom, reduce_mom, by_col),
+        ]
+    )
+    gram = lax.psum_scatter(grams, "ns", scatter_dimension=0, tiled=True)[0]
+    factor = lax.rsqrt(jnp.trace(gram) + SCHULZ_EPSILON)
+    chain = schulz_chain(gram * (factor * factor)) * factor
+    chains = lax.all_gather(chain, "ns", axis=0)
+    left = (((1,), (0,)), ((), ()))
+    right = (((1,), (1,)), ((), ()))
+    project_new = muon_weight(project_weight, precise(chains[0], project_mom, left), 3 * D)
+    output_new = muon_weight(output_weight, precise(output_mom, chains[1], right), D)
+    expand_new = muon_weight(expand_weight, precise(chains[2], expand_mom, left), FF)
+    reduce_new = muon_weight(reduce_weight, precise(reduce_mom, chains[3], right), FF)
+
+    gain_new, gain_one, gain_two = adam_update(
+        norm_gain, norm_gain_first, norm_gain_second, gain_grad, step_count
+    )
+    shift_new, shift_one, shift_two = adam_update(
+        norm_bias, norm_bias_first, norm_bias_second, shift_grad, step_count
+    )
+    pbias_new, pbias_one, pbias_two = adam_update(
+        project_bias, project_bias_first, project_bias_second, project_bias_grad, step_count
+    )
+    obias_new, obias_one, obias_two = adam_update(
+        output_bias, output_bias_first, output_bias_second, cotangent_total, step_count
+    )
+    ebias_new, ebias_one, ebias_two = adam_update(
+        expand_bias, expand_bias_first, expand_bias_second, expand_bias_grad, step_count
+    )
+    rbias_new, rbias_one, rbias_two = adam_update(
+        reduce_bias, reduce_bias_first, reduce_bias_second, cotangent_total, step_count
+    )
+    return (
+        layer_output,
+        input_grad,
+        gain_grad,
+        shift_grad,
+        project_grad,
+        project_bias_grad,
+        output_grad,
+        cotangent_total,
+        expand_grad,
+        expand_bias_grad,
+        reduce_grad,
+        cotangent_total,
+        gain_new,
+        shift_new,
+        project_new,
+        pbias_new,
+        output_new,
+        obias_new,
+        expand_new,
+        ebias_new,
+        reduce_new,
+        rbias_new,
+        project_new.astype(jnp.bfloat16),
+        output_new.astype(jnp.bfloat16),
+        expand_new.astype(jnp.bfloat16),
+        reduce_new.astype(jnp.bfloat16),
+        project_mom,
+        output_mom,
+        expand_mom,
+        reduce_mom,
+        gain_one,
+        gain_two,
+        shift_one,
+        shift_two,
+        pbias_one,
+        pbias_two,
+        obias_one,
+        obias_two,
+        ebias_one,
+        ebias_two,
+        rbias_one,
+        rbias_two,
+    )
+
+
 def solution(mesh):
     return jax.shard_map(
-        per_device,
+        functools.partial(per_device, dict(mesh.shape)),
         mesh=mesh,
         in_specs=(
             P(("rep", "fsdp", "ns"), None),

time: 3260 us -> 1430 us (0.44)
  waiting for transfers between devices: 2220 us -> 778 us
  matrix products: 622 us -> 303 us
  Pallas kernels: 0 us -> 154 us
  local copies, waits for them, and re-layouts: 193 us -> 64.5 us
  starting transfers between devices: 10.8 us -> 76.9 us
  blocking collectives: 59.9 us -> 0 us
  other arithmetic: 84.8 us -> 47.6 us
  loops' own time: 32.6 us -> 0 us
    reduce_scatter x7 -> x3, waiting for transfers between devices: 1230 us -> 305 us  [the longest x1 171 us: split_heads(): lax.psum_scatter(branch.astype(low), ('fsdp', 'ns'), scatter_dimension=0,...]
    psum x7 -> x1, waiting for transfers between devices: 686 us -> 128 us  [split_heads(): lax.psum((gain_term, shift_term, cotangent_sum, project_bias_part, expand...]
    dot_general x81 -> x42, matrix products: 622 us -> 301 us  [the longest x4 67.4 us: dot_nt(): lax.dot_general(left, right, (((1,), (1,)), ((), ())), preferred_element_...]
    all_gather x7 -> x3, waiting for transfers between devices: 307 us -> 0.02 us  [the longest x1 0.01 us: split_heads(): chains = lax.all_gather(chain, 'ns', axis=0)]
    all_to_all x2 -> x8, waiting for transfers between devices: 0.01 us -> 246 us  [exchange(): lax.all_to_all(pieces, 'fsdp', split_axis=0, concat_axis=0, tiled=True)]
    pallas_call x0 -> x4, Pallas kernels: none -> 154 us  [the longest x1 69.3 us: attend_back(): pl.pallas_call(attend_back_body, grid_spec=pltpu.PrefetchScalarGridSpec(n...]
    ppermute x0 -> x4, waiting for transfers between devices: none -> 98.3 us  [both_packs(): lax.ppermute(shard, 'rep', [(0, 1), (1, 0)])]
    all_to_all x2 -> x0, blocking collectives: 59.9 us -> none  [the longest x1 31.9 us: per_device(): lax.all_to_all(tokens[source_row], 'fsdp', split_axis=0, concat_axis=0, t...]
  transfers between devices with their start and end apart: 23 -> 19, of which waited for: 18 -> 13; matrix products, arithmetic and copies ran while one was open for 19% -> 23% of each run, Pallas kernels for 0% -> 11%
where the time goes in v1:
time: 1430 us; the launch traced here: 1440 us
  waiting for transfers between devices  778 us (54%)
  matrix products  303 us (21%)
  Pallas kernels  154 us (11%)
  starting transfers between devices  76.9 us (5%)
  local copies, waits for them, and re-layouts  64.5 us (5%)
  other arithmetic  47.6 us (3%)
  between operations  16.6 us (1%)
    all_to_all x8, waiting for transfers between devices, exchange(): lax.all_to_all(pieces, 'fsdp', split_axis=0, concat_axis=0, tiled=True)  246 us
    reduce_scatter x1, waiting for transfers between devices, split_heads(): lax.psum_scatter(branch.astype(low), ('fsdp', 'ns'), scatter_dimension=0,...  171 us
    psum x1, waiting for transfers between devices, split_heads(): lax.psum((gain_term, shift_term, cotangent_sum, project_bias_part, expand...  128 us
    ppermute x4, waiting for transfers between devices, both_packs(): lax.ppermute(shard, 'rep', [(0, 1), (1, 0)])  98.3 us
    reduce_scatter x1, waiting for transfers between devices, split_heads(): lax.psum_scatter(d_normed_part.astype(low), ('fsdp', 'ns'), scatter_dimen...  87.8 us
    pallas_call x1, Pallas kernels, attend_back(): pl.pallas_call(attend_back_body, grid_spec=pltpu.PrefetchScalarGridSpec(n...  69.3 us
    dot_general x4, matrix products, dot_nt(): lax.dot_general(left, right, (((1,), (1,)), ((), ())), preferred_element_...  67.4 us
    pallas_call x1, Pallas kernels, attend(): pl.pallas_call(attend_body, grid_spec=pltpu.PrefetchScalarGridSpec(num_sc...  58.2 us
  transfers between devices with their start and end apart: 19, of which 13 were waited for; matrix products, arithmetic and copies ran while one was open for 23% of the time, Pallas kernels for 11%

profile of v1, /device:TPU:0, one launch (start us, length us, event | category | flops | bytes accessed | tf_op | source)
XLA Modules:
  0.0 1440.6 jit_solution(13719497173351725517)
XLA Ops:
  17.6 6.3 all-to-all-start.1
  26.4 26.3 %all-to-all-done.1 = bf16[4,128,512]{2,1,0:T(8,128)(2,1)} async-done(((bf16[4,128,512]{2,1,0:T(8,128)(2,1)}), bf16[4,128,512]{2,1,0:T(8,128)(2,1)}, u32[]{:S(2)}, u32[]{:S(2)}) %all-to-all-start.1) | async-done | bytes 524320 | tf_op jit(solution)/shard_map/all_to_all | solution.py:930
  52.7 4.0 all-to-all-start
  56.8 3.8 convert_element_type.131
  60.5 45.5 %all-to-all-done = bf16[4,512,384]{1,2,0:T(8,128)(2,1)S(1)} async-done(((bf16[4,512,384]{1,2,0:T(8,128)(2,1)}), bf16[4,512,384]{1,2,0:T(8,128)(2,1)S(1)}, u32[]{:S(2)}, u32[]{:S(2)}) %all-to-all-start) | async-done | bytes 1572896 | tf_op jit(solution)/shard_map/all_to_all | solution.py:930
  107.2 3.6 all-to-all-start.3
  110.8 4.6 copy.143
  115.4 95.9 %all-to-all-done.3 = bf16[4,512,512]{2,1,0:T(8,128)(2,1)S(1)} async-done(((bf16[4,512,512]{2,1,0:T(8,128)(2,1)}), bf16[4,512,512]{2,1,0:T(8,128)(2,1)S(1)}, u32[]{:S(2)}, u32[]{:S(2)}) %all-to-all-start.3) | async-done | bytes 2097184 | tf_op jit(solution)/shard_map/all_to_all | solution.py:930
  211.3 4.9 all-to-all-start.2
  217.5 9.4 multiply_sine_fusion
  228.3 7.7 concatenate.10.cosine_ref
  236.9 9.1 concatenate.11.sine_ref
  247.5 2.8 copy.139
  252.7 46.2 %all-to-all-done.2 = bf16[4,512,512]{1,2,0:T(8,128)(2,1)} async-done(((bf16[4,512,512]{1,2,0:T(8,128)(2,1)}), bf16[4,512,512]{1,2,0:T(8,128)(2,1)}, u32[]{:S(2)}, u32[]{:S(2)}) %all-to-all-start.2) | async-done | bytes 2097184 | tf_op jit(solution)/shard_map/all_to_all | solution.py:930
  298.9 4.1 copy.144
  303.0 15.8 %convolution_add_fusion = f32[4096,384]{1,0:T(8,128)} fusion(bf16[4096,2048]{1,0:T(8,128)(2,1)} %all-gather.5.cloned.1.call-done, bf16[2048,384]{1,0:T(8,128)(2,1)S(1)} %bitcast.164, f32[384]{0:T(512)S(1)} %add.328), kind=kOutput, calls=%fused_computation.21 | convolution fusion | flops 6444023808 | bytes 24643072 | tf_op jit(solution)/shard_map/dot_general | solution.py:970
  318.8 12.9 rope.1
  331.7 58.2 %attend.1 = (bf16[4,4,4,64,128]{4,3,2,1,0:T(8,128)(2,1)}, f32[8,4096]{1,0:T(8,128)}) custom-call(s32[4]{0:T(128)} %bitcast.183, bf16[4096,128]{1,0:T(8,128)(2,1)} %get-tuple-element.54.q_ref, bf16[4096,128]{1,0:T(8,128)(2,1)} %get-tuple-element.55.k_ref, bf16[128,4096]{1,0:T(8,128)(2,1)} %get-tuple-element.56.vt_ref), custom_call_target="tpu_custom_call" | custom-call | flops 4294967296 | bytes 5242880 | tf_op jit(solution)/shard_map/attend/pallas_call | solution.py:352
  390.0 8.5 convolution_convert_fusion.7
  399.3 15.3 %all-to-all-start.5 = ((bf16[4,128,512]{2,1,0:T(8,128)(2,1)}), bf16[4,128,512]{2,1,0:T(8,128)(2,1)S(1)}, u32[]{:S(2)}, u32[]{:S(2)}) async-start(bf16[4,128,512]{2,1,0:T(8,128)(2,1)} %bitcast.153), calls=%async_computation.7 | async-start | bytes 1048576 | tf_op jit(solution)/shard_map/all_to_all | solution.py:930
  414.6 9.2 convolution_convert_fusion
  423.8 69.3 %attend_back.1 = (f32[4096,128]{1,0:T(8,128)}, f32[4096,128]{1,0:T(8,128)}, f32[4096,128]{1,0:T(8,128)}) custom-call(s32[4]{0:T(128)} %bitcast.184, bf16[4096,128]{1,0:T(8,128)(2,1)} %get-tuple-element.54.q_ref, bf16[4,4,4,64,128]{4,3,2,1,0:T(8,128)(2,1)} %bitcast.185, f32[8,4096]{1,0:T(8,128)} %get-tuple-element.58.stat_ref, ...), custom_call_target="tpu_custom_call" | custom-call | flops 8589934592 | bytes 12582912 | tf_op jit(solution)/shard_map/attend_back/pallas_call | solution.py:388
  493.1 13.4 unrope.1
  506.5 14.6 %fusion.103 = f32[4096,512]{1,0:T(8,128)} fusion(bf16[4096,2048]{1,0:T(8,128)(2,1)} %all-gather.5.cloned.1.call-done, bf16[2048,512]{1,0:T(8,128)(2,1)S(1)} %bitcast.175), kind=kOutput, calls=%fused_computation.204 | convolution fusion | flops 8589934592 | bytes 27262976 | tf_op jit(solution)/shard_map/dot_general | solution.py:974
  521.1 12.4 convolution_convert_fusion.3
  535.9 4.8 all-to-all-start.4
  540.7 15.2 %convolution_convert_fusion.1 = bf16[512,2048]{1,0:T(8,128)(2,1)S(1)} fusion(bf16[4096,2048]{1,0:T(8,128)(2,1)} %all-gather.7.cloned.1.call-done, f32[4096,512]{1,0:T(8,128)} %fusion.103, f32[512]{0:T(512)S(1)} %dynamic_slice.13), kind=kOutput, calls=%fused_computation.42 | convolution fusion | flops 8611954688 | bytes 27265024 | tf_op jit(solution)/shard_map/dot_general | solution.py:1006
  557.4 19.6 %all-to-all-done.4 = bf16[4,512,384]{2,1,0:T(8,128)(2,1)S(1)} async-done(((bf16[4,512,384]{2,1,0:T(8,128)(2,1)}), bf16[4,512,384]{2,1,0:T(8,128)(2,1)S(1)}, u32[]{:S(2)}, u32[]{:S(2)}) %all-to-all-start.4) | async-done | bytes 1572896 | tf_op jit(solution)/shard_map/all_to_all | solution.py:930
  578.1 4.0 all-to-all-start.7
  582.2 19.5 %convert_reduce_fusion = (f32[512]{0:T(512)S(1)}, bf16[4096,512]{1,0:T(8,128)(2,1)S(1)}) fusion(bf16[4096,2048]{1,0:T(8,128)(2,1)} %all-gather.7.cloned.1.call-done, bf16[512,2048]{0,1:T(8,128)(2,1)} %bitcast.172, f32[4096,512]{1,0:T(8,128)} %fusion.103, f32[512]{0:T(512)S(1)} %dynamic_slice.13), kind=kOutput, calls=%fused_computation.20 | convolution fusion | flops 8636071936 | bytes 31461376 | tf_op jit(solution)/shard_map/dot_general | solution.py:107
  603.7 13.5 convolution_convert_fusion.2
  617.1 12.7 all-to-all-done.7
  631.2 3.6 all-to-all-start.6
  637.4 25.3 %collective-permute-start = (bf16[512,1536]{0,1:T(8,128)(2,1)}, bf16[512,1536]{0,1:T(8,128)(2,1)}, u32[]{:S(2)}, u32[]{:S(2)}) collective-permute-start(bf16[512,1536]{0,1:T(8,128)(2,1)} %bitcast.162), channel_id=1, source_target_pairs={{0,16},{16,0},{1,17},{17,1},{2,18},{18,2},{3,19},{19,3},{4,20},{20... | collective-permute-start | bytes 4718600 | tf_op jit(solution)/shard_map/ppermute | solution.py:1011
  664.8 3.7 copy.151
  668.5 41.0 %collective-permute-done.1 = bf16[512,512]{1,0:T(8,128)(2,1)S(1)} collective-permute-done((bf16[512,512]{1,0:T(8,128)(2,1)S(1)}, bf16[512,512]{1,0:T(8,128)(2,1)S(1)}, u32[]{:S(2)}, u32[]{:S(2)}) %collective-permute-start.1) | collective-permute-done | bytes 524320 | tf_op jit(solution)/shard_map/ppermute | solution.py:1011
  712.9 2.9 convolution_bitcast_fusion.2
  718.1 5.1 multiply_add_fusion.3
  723.2 5.2 convolution_bitcast_fusion.3
  728.3 26.2 %collective-permute-done.3 = bf16[2048,512]{1,0:T(8,128)(2,1)} collective-permute-done((bf16[2048,512]{1,0:T(8,128)(2,1)}, bf16[2048,512]{1,0:T(8,128)(2,1)}, u32[]{:S(2)}, u32[]{:S(2)}) %collective-permute-start.3) | collective-permute-done | bytes 2097184 | tf_op jit(solution)/shard_map/ppermute | solution.py:1011
  754.5 4.7 multiply_add_fusion.1
  759.2 7.5 convolution_bitcast_fusion
  766.7 31.1 %collective-permute-done.2 = bf16[512,2048]{1,0:T(8,128)(2,1)S(1)} collective-permute-done((bf16[512,2048]{1,0:T(8,128)(2,1)S(1)}, bf16[512,2048]{1,0:T(8,128)(2,1)S(1)}, u32[]{:S(2)}, u32[]{:S(2)}) %collective-permute-start.2) | collective-permute-done | bytes 2097184 | tf_op jit(solution)/shard_map/ppermute | solution.py:1011
  797.8 3.2 multiply_add_fusion.2
  801.0 7.1 convolution_bitcast_fusion.1
  810.7 46.0 %reduce-scatter.8.cloned.1.call-done = f32[1,512,512]{2,1,0:T(8,128)} async-done(((f32[4,512,512]{2,1,0:T(8,128)}), f32[1,512,512]{2,1,0:T(8,128)}) %reduce-scatter.8.cloned.1.call-update) | async-done | bytes 1048592 | tf_op jit(solution)/shard_map/reduce_scatter | solution.py:1078
  859.3 4.0 fusion.33
  863.3 3.1 fusion.47
  893.1 2.8 convolution_multiply_fusion.2
  896.0 18.7 %fusion.104 = f32[4096,2048]{1,0:T(8,128)} fusion(bf16[4096,512]{1,0:T(8,128)(2,1)} %copy-done.61, bf16[2048,512]{1,0:T(8,128)(2,1)} %bitcast.174), kind=kOutput, calls=%fused_computation.205 | convolution fusion | flops 8589934592 | bytes 39845888 | tf_op jit(solution)/shard_map/dot_general | solution.py:107
  914.7 20.0 %add_convert_fusion = bf16[4096,2048]{1,0:T(8,128)(2,1)} fusion(f32[4096,2048]{1,0:T(8,128)} %fusion.104, bf16[4096,384]{1,0:T(8,128)(2,1)} %bitcast.166, bf16[2048,384]{1,0:T(8,128)(2,1)S(1)} %bitcast.165), kind=kOutput, calls=%fused_computation | convolution fusion | flops 6459228160 | bytes 55050240 | tf_op jit(solution)/shard_map/dot_general | solution.py:107
  935.1 23.3 %fusion.102 = f32[4096,2048]{1,0:T(8,128)} fusion(bf16[4096,128]{1,0:T(8,128)(2,1)} %bitcast.155, bf16[128,2048]{0,1:T(8,128)(2,1)} %bitcast.169), kind=kOutput, calls=%fused_computation.203 | convolution fusion | flops 2147483648 | bytes 35127296 | tf_op jit(solution)/shard_map/dot_general | solution.py:976
  958.3 26.2 %add_convert_fusion.1 = bf16[4096,2048]{1,0:T(8,128)(2,1)} fusion(f32[4096,2048]{1,0:T(8,128)} %fusion.102, bf16[512,2048]{0,1:T(8,128)(2,1)} %bitcast.173, f32[4096,512]{1,0:T(8,128)} %fusion.103, f32[512]{0:T(512)S(1)} %dynamic_slice.13), kind=kOutput, calls=%fused_computation.1 | convolution fusion | flops 8627683328 | bytes 60819456 | tf_op jit(solution)/shard_map/dot_general | solution.py:976
  988.8 3.5 copy.152
  992.4 5.2 fusion.99
  997.6 8.7 fusion.98
  1006.4 9.2 fusion.100
  1015.6 9.3 fusion.101
  1024.9 87.8 %reduce-scatter.6.cloned.1.call-done = bf16[256,2048]{1,0:T(8,128)(2,1)} async-done(((bf16[4096,2048]{1,0:T(8,128)(2,1)}), bf16[256,2048]{1,0:T(8,128)(2,1)}) %reduce-scatter.6.cloned.1.call-update) | async-done | bytes 1048592 | tf_op jit(solution)/shard_map/reduce_scatter | solution.py:991
  1115.2 2.8 fusion.22
  1118.2 3.7 convolution_convert_fusion.4
  1121.9 171.2 %reduce-scatter.4.cloned.1.call-done = bf16[256,2048]{1,0:T(8,128)(2,1)} async-done(((bf16[4096,2048]{1,0:T(8,128)(2,1)}), bf16[256,2048]{1,0:T(8,128)(2,1)}) %reduce-scatter.4.cloned.1.call-update) | async-done | bytes 1048592 | tf_op jit(solution)/shard_map/reduce_scatter | solution.py:979
  1293.1 2.8 convolution_convert_fusion.6
  1295.9 128.2 %all-reduce.3.cloned.1.call-done = (f32[2048]{0:T(1024)}, f32[2048]{0:T(1024)}, f32[6144]{0:T(1024)}, f32[2048]{0:T(1024)}, f32[8192]{0:T(1024)}) async-done(((f32[2048]{0:T(1024)}, f32[2048]{0:T(1024)}, f32[6144]{0:T(1024)}, f32[2048]{0:T(1024)}, f32[8192]{0:T(1024)}), (f32[2048]{0:T(1024)}, f32[2048]{0:T(1024)}, f32[6144]{0:T(1024)}, f32[2048]{0:T(1024)}, f32[8192]{0:T(1024)})) %all-reduce.3.cloned.1.call-update) | async-done | bytes 81936 | tf_op jit(solution)/shard_map/psum | solution.py:1052
  (213 shorter events, 87.8 us)
Async XLA Ops:
  7.2 6.0 copy-start
  7.3 295.7 %all-gather.5.cloned.1.call-start = ((), (), s32[]{:S(2)}) async-start(), calls=%async_computation.11 | async-start | bytes 17825792 | tf_op jit(solution)/shard_map/all_gather | solution.py:926
  13.2 376.8 %all-gather.7.cloned.1.call-start = ((), (), s32[]{:S(2)}) async-start(), calls=%async_computation.13 | async-start | bytes 17825792 | tf_op jit(solution)/shard_map/all_gather | solution.py:927
  15.3 8.6 copy-start.11
  17.6 35.2 %all-to-all-start.1 = ((bf16[4,128,512]{2,1,0:T(8,128)(2,1)}), bf16[4,128,512]{2,1,0:T(8,128)(2,1)}, u32[]{:S(2)}, u32[]{:S(2)}) async-start(bf16[4,128,512]{2,1,0:T(8,128)(2,1)} %bitcast.170), calls=%async_computation.1 | async-start | bytes 1048576 | tf_op jit(solution)/shard_map/all_to_all | solution.py:930
  52.7 53.3 %all-to-all-start = ((bf16[4,512,384]{1,2,0:T(8,128)(2,1)}), bf16[4,512,384]{1,2,0:T(8,128)(2,1)S(1)}, u32[]{:S(2)}, u32[]{:S(2)}) async-start(bf16[4,512,384]{1,2,0:T(8,128)(2,1)} %fusion.25), calls=%async_computation | async-start | bytes 3145728 | tf_op jit(solution)/shard_map/all_to_all | solution.py:930
  107.2 104.2 %all-to-all-start.3 = ((bf16[4,512,512]{2,1,0:T(8,128)(2,1)}), bf16[4,512,512]{2,1,0:T(8,128)(2,1)S(1)}, u32[]{:S(2)}, u32[]{:S(2)}) async-start(bf16[4,512,512]{2,1,0:T(8,128)(2,1)} %bitcast.14), calls=%async_computation.3 | async-start | bytes 4194304 | tf_op jit(solution)/shard_map/all_to_all | solution.py:930
  110.8 106.4 %copy-start.60 = (s32[1,4]{1,0:T(1,128)S(1)}, s32[1,4]{1,0:T(1,128)}, u32[]{:S(2)}) copy-start(s32[1,4]{1,0:T(1,128)} %param.34) | copy-start | bytes 52
  211.3 6.2 copy-start.13
  211.3 87.5 %all-to-all-start.2 = ((bf16[4,512,512]{1,2,0:T(8,128)(2,1)}), bf16[4,512,512]{1,2,0:T(8,128)(2,1)}, u32[]{:S(2)}, u32[]{:S(2)}) async-start(bf16[4,512,512]{1,2,0:T(8,128)(2,1)} %bitcast.12), calls=%async_computation.2 | async-start | bytes 4194304 | tf_op jit(solution)/shard_map/all_to_all | solution.py:930
  247.5 167.1 %copy-start.27 = (bf16[128,4,512]{0,2,1:T(8,128)(2,1)}, bf16[128,4,512]{0,2,1:T(8,128)(2,1)S(1)}, u32[]{:S(2)}) copy-start(bf16[128,4,512]{0,2,1:T(8,128)(2,1)S(1)} %copy.142) | copy-start | bytes 1572868
  252.7 50.3 %copy-start.20 = (bf16[4,512,384]{2,1,0:T(8,128)(2,1)S(1)}, bf16[4,512,384]{2,1,0:T(8,128)(2,1)}, u32[]{:S(2)}) copy-start(bf16[4,512,384]{2,1,0:T(8,128)(2,1)} %copy.139) | copy-start | bytes 4718596
  399.3 136.7 %all-to-all-start.5 = ((bf16[4,128,512]{2,1,0:T(8,128)(2,1)}), bf16[4,128,512]{2,1,0:T(8,128)(2,1)S(1)}, u32[]{:S(2)}, u32[]{:S(2)}) async-start(bf16[4,128,512]{2,1,0:T(8,128)(2,1)} %bitcast.153), calls=%async_computation.7 | async-start | bytes 1048576 | tf_op jit(solution)/shard_map/all_to_all | solution.py:930
  493.1 13.4 copy-start.28
  506.5 14.6 %copy-start.26 = (bf16[4,4,4,64,384]{4,3,2,1,0:T(8,128)(2,1)S(1)}, bf16[4,4,4,64,384]{4,3,2,1,0:T(8,128)(2,1)}, u32[]{:S(2)}) copy-start(bf16[4,4,4,64,384]{4,3,2,1,0:T(8,128)(2,1)} %get-tuple-element.64) | copy-start | bytes 9437188
  535.9 41.1 %all-to-all-start.4 = ((bf16[4,512,384]{2,1,0:T(8,128)(2,1)}), bf16[4,512,384]{2,1,0:T(8,128)(2,1)S(1)}, u32[]{:S(2)}, u32[]{:S(2)}) async-start(bf16[4,512,384]{2,1,0:T(8,128)(2,1)} %fusion.50), calls=%async_computation.6 | async-start | bytes 3145728 | tf_op jit(solution)/shard_map/all_to_all | solution.py:930
  578.1 51.7 %all-to-all-start.7 = ((bf16[4,512,512]{2,1,0:T(8,128)(2,1)}), bf16[4,512,512]{2,1,0:T(8,128)(2,1)S(1)}, u32[]{:S(2)}, u32[]{:S(2)}) async-start(bf16[4,512,512]{2,1,0:T(8,128)(2,1)} %bitcast.151), calls=%async_computation.9 | async-start | bytes 4194304 | tf_op jit(solution)/shard_map/all_to_all | solution.py:930
  631.2 84.6 %all-to-all-start.6 = ((bf16[4,512,512]{2,1,0:T(8,128)(2,1)}), bf16[4,512,512]{2,1,0:T(8,128)(2,1)S(1)}, u32[]{:S(2)}, u32[]{:S(2)}) async-start(bf16[4,512,512]{2,1,0:T(8,128)(2,1)} %bitcast.176), calls=%async_computation.8 | async-start | bytes 4194304 | tf_op jit(solution)/shard_map/all_to_all | solution.py:930
  634.8 221.9 %reduce-scatter.8.cloned.1.call-start = ((), (), s32[]{:S(2)}) async-start(), calls=%async_computation.15 | async-start | bytes 5242880 | tf_op jit(solution)/shard_map/reduce_scatter | solution.py:1078
  637.4 80.7 %collective-permute-start = (bf16[512,1536]{0,1:T(8,128)(2,1)}, bf16[512,1536]{0,1:T(8,128)(2,1)}, u32[]{:S(2)}, u32[]{:S(2)}) collective-permute-start(bf16[512,1536]{0,1:T(8,128)(2,1)} %bitcast.162), channel_id=1, source_target_pairs={{0,16},{16,0},{1,17},{17,1},{2,18},{18,2},{3,19},{19,3},{4,20},{20... | collective-permute-start | bytes 4718600 | tf_op jit(solution)/shard_map/ppermute | solution.py:1011
  662.8 46.7 %collective-permute-start.1 = (bf16[512,512]{1,0:T(8,128)(2,1)S(1)}, bf16[512,512]{1,0:T(8,128)(2,1)S(1)}, u32[]{:S(2)}, u32[]{:S(2)}) collective-permute-start(bf16[512,512]{1,0:T(8,128)(2,1)S(1)} %bitcast.178), channel_id=1, source_target_pairs={{0,16},{16,0},{1,17},{17,1},{2,18},{18,2},{3,19},{19,3},{4,20},{20... | collective-permute-start | bytes 1572872 | tf_op jit(solution)/shard_map/ppermute | solution.py:1011
  662.8 91.7 %collective-permute-start.3 = (bf16[2048,512]{1,0:T(8,128)(2,1)}, bf16[2048,512]{1,0:T(8,128)(2,1)}, u32[]{:S(2)}, u32[]{:S(2)}) collective-permute-start(bf16[2048,512]{1,0:T(8,128)(2,1)} %bitcast.158), channel_id=1, source_target_pairs={{0,16},{16,0},{1,17},{17,1},{2,18},{18,2},{3,19},{19,3},{4,20},{20... | collective-permute-start | bytes 6291464 | tf_op jit(solution)/shard_map/ppermute | solution.py:1011
  716.0 81.8 %collective-permute-start.2 = (bf16[512,2048]{1,0:T(8,128)(2,1)S(1)}, bf16[512,2048]{1,0:T(8,128)(2,1)S(1)}, u32[]{:S(2)}, u32[]{:S(2)}) collective-permute-start(bf16[512,2048]{1,0:T(8,128)(2,1)S(1)} %bitcast.159), channel_id=1, source_target_pairs={{0,16},{16,0},{1,17},{17,1},{2,18},{18,2},{3,19},{19,3},{4,20},{20... | collective-permute-start | bytes 6291464 | tf_op jit(solution)/shard_map/ppermute | solution.py:1011
  723.2 31.4 %copy-start.16 = (bf16[4,512,512]{2,1,0:T(8,128)(2,1)S(1)}, bf16[4,512,512]{2,1,0:T(8,128)(2,1)}, u32[]{:S(2)}) copy-start(bf16[4,512,512]{2,1,0:T(8,128)(2,1)} %copy-done.15) | copy-start | bytes 6291460
  723.2 31.4 %copy-start.22 = (f32[2048,512]{1,0:T(8,128)S(1)}, f32[2048,512]{1,0:T(8,128)}, u32[]{:S(2)}) copy-start(f32[2048,512]{1,0:T(8,128)} %param.49) | copy-start | bytes 12582916
  759.2 7.5 copy-start.6
  759.2 38.6 %copy-start.23 = (f32[512,2048]{1,0:T(8,128)S(1)}, f32[512,2048]{1,0:T(8,128)}, u32[]{:S(2)}) copy-start(f32[512,2048]{1,0:T(8,128)} %param.48) | copy-start | bytes 12582916
  801.0 7.1 copy-start.2
  801.0 7.1 copy-start.24
  810.6 181.8 %all-gather.9.cloned.1.call-start = ((), (), s32[]{:S(2)}) async-start(), calls=%async_computation.16 | async-start | bytes 5242880 | tf_op jit(solution)/shard_map/all_gather | solution.py:1081
  896.0 216.7 %reduce-scatter.6.cloned.1.call-start = ((), (), s32[]{:S(2)}) async-start(), calls=%async_computation.14 | async-start | bytes 17825792 | tf_op jit(solution)/shard_map/reduce_scatter | solution.py:991
  896.0 18.7 %copy-start.21 = (bf16[4,512,384]{2,1,0:T(8,128)(2,1)S(1)}, bf16[4,512,384]{2,1,0:T(8,128)(2,1)}, u32[]{:S(2)}) copy-start(bf16[4,512,384]{2,1,0:T(8,128)(2,1)} %copy.139) | copy-start | bytes 4718596
  934.8 358.3 %reduce-scatter.4.cloned.1.call-start = ((), (), s32[]{:S(2)}) async-start(), calls=%async_computation.12 | async-start | bytes 17825792 | tf_op jit(solution)/shard_map/reduce_scatter | solution.py:979
  984.6 439.5 %all-reduce.3.cloned.1.call-start = ((), (), s32[]{:S(2)}) async-start(), calls=%async_computation.17 | async-start | bytes 163840 | tf_op jit(solution)/shard_map/psum | solution.py:1052
  986.2 6.2 copy-start.32
  992.4 13.9 copy-start.25
  997.6 8.7 copy-start.3
  997.6 8.7 copy-start.8
  1006.3 9.2 copy-start.7
  1006.4 9.2 copy-start.9
  1015.6 97.1 %copy-start.5 = (f32[256,2048]{1,0:T(8,128)S(1)}, f32[256,2048]{1,0:T(8,128)}, u32[]{:S(2)}) copy-start(f32[256,2048]{1,0:T(8,128)} %copy-done.4) | copy-start | bytes 6291460
  1015.6 97.1 %copy-start.30 = (f32[2048]{0:T(1024)S(1)}, f32[2048]{0:T(1024)}, u32[]{:S(2)}) copy-start(f32[2048]{0:T(1024)} %param.36) | copy-start | bytes 24580
  1015.6 97.1 %copy-start.38 = (f32[256]{0:T(256)S(1)}, f32[256]{0:T(256)}, u32[]{:S(2)}) copy-start(f32[256]{0:T(256)} %copy-done.37) | copy-start | bytes 3076
  1015.6 99.6 %copy-start.45 = (f32[256]{0:T(256)S(1)}, f32[256]{0:T(256)}, u32[]{:S(2)}) copy-start(f32[256]{0:T(256)} %copy-done.44) | copy-start | bytes 3076
  1015.6 99.6 %copy-start.47 = (f32[256]{0:T(256)S(1)}, f32[256]{0:T(256)}, u32[]{:S(2)}) copy-start(f32[256]{0:T(256)} %copy-done.46) | copy-start | bytes 3076
  1024.9 93.1 %copy-start.40 = (s32[256]{0:T(256)S(1)}, s32[256]{0:T(256)}, u32[]{:S(2)}) copy-start(s32[256]{0:T(256)} %copy-done.39) | copy-start | bytes 3076
  1115.2 177.9 %copy-start.35 = (f32[2048]{0:T(1024)S(1)}, f32[2048]{0:T(1024)}, u32[]{:S(2)}) copy-start(f32[2048]{0:T(1024)} %param.45) | copy-start | bytes 24580
  1115.2 177.9 %copy-start.36 = (f32[2048]{0:T(1024)S(1)}, f32[2048]{0:T(1024)}, u32[]{:S(2)}) copy-start(f32[2048]{0:T(1024)} %param.41) | copy-start | bytes 24580
  1118.0 306.1 %copy-start.41 = (f32[1536]{0:T(1024)S(1)}, f32[1536]{0:T(1024)}, u32[]{:S(2)}) copy-start(f32[1536]{0:T(1024)} %param.39) | copy-start | bytes 18436
  1118.0 306.1 %copy-start.52 = (f32[1536]{0:T(1024)S(1)}, f32[1536]{0:T(1024)}, u32[]{:S(2)}) copy-start(f32[1536]{0:T(1024)} %param.54) | copy-start | bytes 18436
  1118.0 306.1 %copy-start.53 = (f32[1536]{0:T(1024)S(1)}, f32[1536]{0:T(1024)}, u32[]{:S(2)}) copy-start(f32[1536]{0:T(1024)} %param.55) | copy-start | bytes 18436
  1118.1 307.5 %copy-start.34 = (f32[2048]{0:T(1024)S(1)}, f32[2048]{0:T(1024)}, u32[]{:S(2)}) copy-start(f32[2048]{0:T(1024)} %param.37) | copy-start | bytes 24580
  1118.1 307.5 %copy-start.48 = (f32[2048]{0:T(1024)S(1)}, f32[2048]{0:T(1024)}, u32[]{:S(2)}) copy-start(f32[2048]{0:T(1024)} %param.52) | copy-start | bytes 24580
  1118.1 307.5 %copy-start.49 = (f32[2048]{0:T(1024)S(1)}, f32[2048]{0:T(1024)}, u32[]{:S(2)}) copy-start(f32[2048]{0:T(1024)} %param.53) | copy-start | bytes 24580
  1118.1 307.5 %copy-start.50 = (f32[2048]{0:T(1024)S(1)}, f32[2048]{0:T(1024)}, u32[]{:S(2)}) copy-start(f32[2048]{0:T(1024)} %param.51) | copy-start | bytes 24580
  1118.1 307.5 %copy-start.51 = (f32[2048]{0:T(1024)S(1)}, f32[2048]{0:T(1024)}, u32[]{:S(2)}) copy-start(f32[2048]{0:T(1024)} %param.50) | copy-start | bytes 24580
  1118.1 308.8 %copy-start.42 = (f32[2048]{0:T(1024)S(1)}, f32[2048]{0:T(1024)}, u32[]{:S(2)}) copy-start(f32[2048]{0:T(1024)} %param.43) | copy-start | bytes 24580
  1118.1 308.8 %copy-start.54 = (f32[2048]{0:T(1024)S(1)}, f32[2048]{0:T(1024)}, u32[]{:S(2)}) copy-start(f32[2048]{0:T(1024)} %param.60) | copy-start | bytes 24580
  1118.1 308.8 %copy-start.55 = (f32[2048]{0:T(1024)S(1)}, f32[2048]{0:T(1024)}, u32[]{:S(2)}) copy-start(f32[2048]{0:T(1024)} %param.61) | copy-start | bytes 24580
  1118.2 308.8 %copy-start.56 = (f32[2048]{0:T(1024)S(1)}, f32[2048]{0:T(1024)}, u32[]{:S(2)}) copy-start(f32[2048]{0:T(1024)} %param.57) | copy-start | bytes 24580
  1118.2 308.8 %copy-start.57 = (f32[2048]{0:T(1024)S(1)}, f32[2048]{0:T(1024)}, u32[]{:S(2)}) copy-start(f32[2048]{0:T(1024)} %param.56) | copy-start | bytes 24580
  1118.2 308.8 %copy-start.58 = (f32[2048]{0:T(1024)S(1)}, f32[2048]{0:T(1024)}, u32[]{:S(2)}) copy-start(f32[2048]{0:T(1024)} %param.59) | copy-start | bytes 24580
  1118.2 308.8 %copy-start.59 = (f32[2048]{0:T(1024)S(1)}, f32[2048]{0:T(1024)}, u32[]{:S(2)}) copy-start(f32[2048]{0:T(1024)} %param.58) | copy-start | bytes 24580
  1118.2 315.3 %copy-start.1 = (bf16[256,2048]{1,0:T(8,128)(2,1)S(1)}, bf16[256,2048]{1,0:T(8,128)(2,1)}, u32[]{:S(2)}) copy-start(bf16[256,2048]{1,0:T(8,128)(2,1)} %param.32) | copy-start | bytes 3145732
  (17 other events, 43.8 us)
Sparse Core Ops, SparseCore 0:
  13.3 207.6 all-gather.4
  223.2 155.7 all-gather.6
  810.8 45.9 reduce-scatter.7
  896.1 34.4 all-gather.8
  934.9 177.7 reduce-scatter.5
  1116.6 176.4 reduce-scatter.3
  1300.7 123.4 all-reduce.2
